TPU v7x, 256 devices: a whole 4x4x8 slice. The times are simulated.
256 devices in a mesh: grp: 4 (over y), chan: 64 (over x, z, core).
Axes of the slice: x: 4, y: 4, z: 8, core: 2. Of those that a mesh axis runs over, the one named last changes fastest.
Arguments:
- generator: bfloat16 [4, 64, 896, 896], P('grp', 'chan'), may hold values from -0.1875 to 0.1875
- hamiltonian: bfloat16 [4, 64, 896, 896], P('grp', 'chan'), may hold values from -6 to 6
- occupation: float32 [4, 64, 896], P('grp', 'chan'), may hold values from -1 to 1
- owner: int32 [4, 64, 49, 1], replicated, may hold values from 0 to 63; in each aligned block of 49 rows (0 to 48, 49 to 97, ..., all dimensions but the last counted through in order) at most 2 rows name the same one
- offset: int32 [4, 64, 49], replicated, may hold values from 0 to 48
Outputs:
- commutator: float32 [4, 64, 896, 896], P('grp', 'chan')
Inputs may be any that keep to these rules, and one draw needn't show every extreme that they name: Among the 49 tiles of one channel, no owner is named more than 2 times; some owner exactly 2 times in some channels. Every owner receives a tile somewhere.
All inputs are finite; a program needn't handle non-finite values.
Results may differ from a plain program's by a relative error of at most 0.0042.
Values may be sent and summed in bfloat16 or wider, within the bound.
No kernel may reach another device: no remote copies, remote signals or barrier semaphores. Data moves between devices by JAX's collectives and lax.ppermute only.
A program may use at most 128 MiB of HBM per device.

v0:
```python
import jax
import jax.numpy as jnp
from jax import lax
from jax.experimental import pallas as pl
from jax.experimental.pallas import tpu as pltpu
from jax.sharding import PartitionSpec as P


TILE = 128
SIDE = 7
BLOCKS = SIDE * SIDE
X, Z, CORE = 4, 8, 2
CHAN = X * Z * CORE
UPPER = 112
LIMIT = 24
PIECE = TILE // (X * CORE)
RELATIVE = [(step, flip) for flip in range(CORE) for step in range(X)]
F32, BF16 = jnp.float32, jnp.bfloat16


SMEM = pl.BlockSpec(memory_space=pltpu.SMEM)
VMEM = pl.BlockSpec(memory_space=pltpu.VMEM)


def chan_of(x, z, core):
    return (x * Z + z) * CORE + core


def z_shift(value, step):
    pairs = [
        (chan_of(x, z, c), chan_of(x, (z + step) % Z, c))
        for x in range(X)
        for z in range(Z)
        for c in range(CORE)
    ]
    return lax.ppermute(value, "chan", pairs)


def x_shift(value, step, flip):
    pairs = [
        (chan_of(x, z, c), chan_of((x + step) % X, z, c ^ flip))
        for x in range(X)
        for z in range(Z)
        for c in range(CORE)
    ]
    return lax.ppermute(value, "chan", pairs)


def exchanged(value):
    return lax.all_to_all(value, "chan", split_axis=0, concat_axis=0, tiled=True)


def kernel_call(body, tables, arrays, outs, scratch=(), cost=(0, 0)):
    return pl.pallas_call(
        body,
        out_shape=outs,
        in_specs=[SMEM] * len(tables) + [VMEM] * len(arrays),
        out_specs=jax.tree.map(lambda _: VMEM, outs),
        scratch_shapes=list(scratch),
        cost_estimate=pl.CostEstimate(flops=cost[0], bytes_accessed=cost[1], transcendentals=0),
        compiler_params=pltpu.CompilerParams(vmem_limit_bytes=LIMIT << 20),
    )(*tables, *arrays)


def tile_at(ref, block):
    row = pl.multiple_of((block // SIDE) * TILE, TILE)
    col = pl.multiple_of((block % SIDE) * TILE, TILE)
    return ref[pl.ds(row, TILE), pl.ds(col, TILE)]


def send_tiles(main_blocks, second_blocks, gen, ham):
    count = second_blocks.shape[0]

    def body(main_table, second_table, gen_ref, ham_ref, main_ref, *second_refs):
        for step in range(count):
            block = second_table[step]
            second_refs[step][0] = tile_at(gen_ref, block)
            second_refs[step][1] = tile_at(ham_ref, block)

        @pl.loop(0, CHAN)
        def _(slot):
            block = main_table[slot]
            main_ref[slot, 0] = tile_at(gen_ref, block)
            main_ref[slot, 1] = tile_at(ham_ref, block)

    outs = [jax.ShapeDtypeStruct((CHAN, 2, TILE, TILE), BF16)]
    outs += [jax.ShapeDtypeStruct((2, TILE, TILE), BF16)] * count
    return kernel_call(body, (main_blocks, second_blocks), (gen, ham), outs)


def direct_tiles(blocks, gen, ham):
    def body(table, gen_ref, ham_ref, out_ref):
        @pl.loop(0, CHAN)
        def _(slot):
            block = table[slot]
            out_ref[slot, 0] = tile_at(gen_ref, block)
            out_ref[slot, 1] = tile_at(ham_ref, block)

    out = jax.ShapeDtypeStruct((CHAN, 2, TILE, TILE), BF16)
    return kernel_call(body, (blocks,), (gen, ham), out)


def placed(main_offsets, second_offsets, main, seconds):
    parts = len(seconds)
    each = seconds[0].shape[0]

    def body(main_table, second_table, main_ref, *refs):
        second_refs, (gen_ref, ham_ref, total) = refs[:parts], refs[parts:]

        @pl.loop(0, BLOCKS)
        def _(block):
            total[block] = jnp.zeros((2, TILE, TILE), F32)

        @pl.loop(0, CHAN)
        def _(slot):
            place = main_table[slot]

            @pl.when(place >= 0)
            def _():
                total[place] += main_ref[slot].astype(F32)

        for part in range(parts):

            @pl.loop(0, each)
            def _(slot):
                place = second_table[part * each + slot]

                @pl.when(place >= 0)
                def _():
                    total[place] += second_refs[part][slot].astype(F32)

        @pl.loop(0, BLOCKS)
        def _(block):
            rows = pl.ds(pl.multiple_of((block // SIDE) * TILE, TILE), TILE)
            cols = pl.ds(pl.multiple_of((block % SIDE) * TILE, TILE), TILE)
            gen_ref[rows, cols] = total[block, 0].astype(BF16)
            ham_ref[rows, cols] = total[block, 1].astype(BF16)

    outs = [jax.ShapeDtypeStruct((SIDE * TILE, SIDE * TILE), BF16)] * 2
    scratch = [pltpu.VMEM((BLOCKS, 2, TILE, TILE), F32)]
    return kernel_call(body, (main_offsets, second_offsets), (main, *seconds), outs, scratch)


def back_tiles(main_offsets, second_offsets, pieces, cross):
    count = len(RELATIVE)

    def body(main_table, second_table, piece_table, cross_ref, upper_ref, lower_ref, *piece_refs):
        @pl.loop(0, CHAN)
        def _(slot):
            tile = tile_at(cross_ref, main_table[slot]).astype(BF16)
            upper_ref[slot] = tile[:UPPER]
            lower_ref[slot] = tile[UPPER:]
            block = second_table[slot]

            @pl.when(block >= 0)
            def _():
                row = (block // SIDE) * TILE
                col = pl.multiple_of((block % SIDE) * TILE, TILE)
                for part in range(count):
                    first = pl.multiple_of(row + piece_table[part] * PIECE, PIECE)
                    rows = cross_ref[pl.ds(first, PIECE), pl.ds(col, TILE)]
                    piece_refs[part][slot] = rows.astype(BF16)

    outs = [
        jax.ShapeDtypeStruct((CHAN, UPPER, TILE), BF16),
        jax.ShapeDtypeStruct((CHAN, TILE - UPPER, TILE), BF16),
    ]
    outs += [jax.ShapeDtypeStruct((CHAN, PIECE, TILE), BF16)] * count
    return kernel_call(body, (main_offsets, second_offsets, pieces), (cross,), outs)


def back_direct(main_offsets, second_offsets, cross):
    def body(main_table, second_table, cross_ref, out_ref):
        @pl.loop(0, CHAN)
        def _(slot):
            out_ref[slot, 0] = tile_at(cross_ref, main_table[slot]).astype(BF16)
            out_ref[slot, 1] = tile_at(cross_ref, second_table[slot]).astype(BF16)

    out = jax.ShapeDtypeStruct((CHAN, 2, TILE, TILE), BF16)
    return kernel_call(body, (main_offsets, second_offsets), (cross,), out)


def joined(choice, lower, routed):
    rows = TILE - UPPER

    def body(table, lower_ref, *refs):
        routed_refs, out_ref = refs[:-1], refs[-1]

        @pl.loop(0, CHAN)
        def _(slot):
            out_ref[slot, :rows] = lower_ref[slot]
            part_of = table[slot]
            for part, ref in enumerate(routed_refs):

                @pl.when(part_of == part)
                def _():
                    out_ref[slot, rows:] = ref[slot]

    out = jax.ShapeDtypeStruct((CHAN, rows + PIECE, TILE), BF16)
    return kernel_call(body, (choice,), (lower, *routed), out)


def gathered(slots, main):
    def body(table, main_ref, out_ref):
        @pl.loop(0, BLOCKS)
        def _(block):
            slot = table[block]

            @pl.when(slot >= 0)
            def _():
                out_ref[block] = main_ref[slot]

    out = jax.ShapeDtypeStruct((BLOCKS, *main.shape[1:]), BF16)
    return kernel_call(body, (slots,), (main,), out)


def in_bands(tiles):
    rows = TILE - UPPER

    def body(tile_ref, upper_ref, lower_ref):
        @pl.loop(0, BLOCKS)
        def _(block):
            tile = tile_ref[block]
            upper_ref[block] = tile[:UPPER]
            lower_ref[block] = tile[UPPER:]

    outs = [
        jax.ShapeDtypeStruct((BLOCKS, UPPER, TILE), BF16),
        jax.ShapeDtypeStruct((BLOCKS + Z * (UPPER // rows), rows, TILE), BF16),
    ]
    return kernel_call(body, (), (tiles,), outs)


def gathered_lower(slots, planes, main):
    rows = TILE - UPPER
    units, pieces = UPPER // rows, rows // PIECE

    def body(table, plane_table, main_ref, out_ref):
        @pl.loop(0, BLOCKS)
        def _(block):
            slot, plane = table[block], plane_table[block]

            @pl.when(slot >= 0)
            def _():
                out_ref[block] = main_ref[slot, :rows]

            @pl.when(slot < 0)
            def _():
                for part in range(pieces):
                    where = part + UPPER // PIECE
                    source = chan_of(where // CORE, plane, where % CORE)
                    out_ref[block, pl.ds(part * PIECE, PIECE)] = main_ref[source, rows:]

        @pl.loop(0, Z)
        def _(plane):
            for unit in range(units):
                for part in range(pieces):
                    where = unit * pieces + part
                    source = chan_of(where // CORE, plane, where % CORE)
                    unit_rows = pl.ds(part * PIECE, PIECE)
                    out_ref[BLOCKS + plane * units + unit, unit_rows] = main_ref[source, rows:]

    out = jax.ShapeDtypeStruct((BLOCKS + Z * units, rows, TILE), BF16)
    return kernel_call(body, (slots, planes), (main,), out)


def assembled(own_planes, partner_planes, ladder, own, partner):
    rows = TILE - UPPER
    units = UPPER // rows

    def tile_of(block, plane, upper, upper_block, lower):
        extra = BLOCKS + jnp.maximum(plane, 0) * units
        late = lower[pl.ds(extra, units)].reshape(UPPER, TILE)
        top = jnp.where(plane >= 0, late, upper[upper_block])
        return jnp.concatenate([top, lower[block]])

    def body(own_table, partner_table, ladder_ref, upper, lower, mirror_upper, mirror_lower, out_ref):
        i = pl.program_id(0)

        @pl.loop(0, SIDE)
        def _(j):
            cols = pl.ds(pl.multiple_of(j * TILE, TILE), TILE)
            here, there = i * SIDE + j, j * SIDE + i
            mine = tile_of(here, own_table[here], upper, j, lower)
            theirs = tile_of(there, partner_table[there], mirror_upper, there, mirror_lower)
            out_ref[:, cols] = ladder_ref[:, cols] + mine.astype(F32) - theirs.T.astype(F32)

    side = SIDE * TILE
    whole = [pl.BlockSpec(a.shape, lambda i: (0, 0, 0)) for a in (own[1], *partner)]
    return pl.pallas_call(
        body,
        grid=(SIDE,),
        out_shape=jax.ShapeDtypeStruct((side, side), F32),
        in_specs=[
            SMEM,
            SMEM,
            pl.BlockSpec((TILE, side), lambda i: (i, 0)),
            pl.BlockSpec((SIDE, UPPER, TILE), lambda i: (i, 0, 0)),
            *whole,
        ],
        out_specs=pl.BlockSpec((TILE, side), lambda i: (i, 0)),
        compiler_params=pltpu.CompilerParams(vmem_limit_bytes=LIMIT << 20),
    )(own_planes, partner_planes, ladder, *own, *partner)


def pair_product(left_a, right_a, left_b, right_b):
    first = jnp.dot(left_a, right_a, preferred_element_type=F32)
    return first - jnp.dot(left_b, right_b, preferred_element_type=F32)


def commutator_by_rows(gen, ham):
    def body(gen_rows, ham_rows, gen_ref, ham_ref, out_ref):
        first = jnp.dot(gen_rows[...], ham_ref[...], preferred_element_type=F32)
        out_ref[...] = first - jnp.dot(ham_rows[...], gen_ref[...], preferred_element_type=F32)

    band = pl.BlockSpec((TILE, SIDE * TILE), lambda i: (i, 0))
    whole = pl.BlockSpec(gen.shape, lambda i: (0, 0))
    return pl.pallas_call(
        body,
        grid=(SIDE,),
        out_shape=jax.ShapeDtypeStruct(gen.shape, F32),
        in_specs=[band, band, whole, whole],
        out_specs=band,
        compiler_params=pltpu.CompilerParams(vmem_limit_bytes=LIMIT << 20),
    )(gen, ham, gen, ham)


def ladder_term(gen_mat, ham_mat, occ_row):
    gen_occ = (gen_mat.astype(F32) * occ_row[None, :]).astype(BF16)
    ham_occ = (ham_mat.astype(F32) * occ_row[None, :]).astype(BF16)
    return pair_product(gen_occ, ham_mat, ham_occ, gen_mat)


def homes_of(owner_map):
    names = jnp.arange(CHAN, dtype=jnp.int32)
    tiles = jnp.sum((owner_map[..., None] == names).astype(jnp.int32), axis=-2)
    double = tiles == 2
    load = jnp.sum(double.astype(jnp.int32), axis=-2)
    mine, other = load[..., :, None], load[..., None, :]
    ahead = (other > mine) | ((other == mine) & (names[None, :] < names[:, None]))
    rank = jnp.sum(ahead.astype(jnp.int32), axis=-1)
    return rank, double


def on_device(generator, hamiltonian, occupation, owner, offset):
    gen_mat, ham_mat, occ_row = generator[0, 0], hamiltonian[0, 0], occupation[0, 0]
    me, grp = lax.axis_index("chan"), lax.axis_index("grp")
    my_x, my_z, my_core = me // (Z * CORE), (me // CORE) % Z, me % CORE
    owner_all = owner[:, :, :, 0]
    owners = lax.dynamic_index_in_dim(owner_all, grp, 0, keepdims=False)
    offsets = lax.dynamic_index_in_dim(offset, grp, 0, keepdims=False)
    names = jnp.arange(CHAN, dtype=jnp.int32)
    blocks = jnp.arange(BLOCKS, dtype=jnp.int32)
    steps = jnp.arange(Z, dtype=jnp.int32)

    def home_of(rank):
        row, col = rank // Z, rank % Z
        return chan_of(row // CORE, col, row % CORE)

    rank, _ = homes_of(owners)
    dest = jnp.sum(jnp.where(owners[:, :, None] == names, home_of(rank), 0), axis=-1)
    alike = (owners[:, None, :] == owners[:, :, None]) & (blocks[None, :] < blocks[:, None])
    later = jnp.any(alike, axis=-1)

    my_dest = lax.dynamic_index_in_dim(dest, me, 0, keepdims=False)
    my_later = lax.dynamic_index_in_dim(later, me, 0, keepdims=False)
    my_plane = (my_dest // CORE) % Z
    to_home = my_dest[None, :] == names[:, None]
    main_blocks = jnp.max(jnp.where(to_home & ~my_later, blocks, 0), axis=1)
    direct_blocks = jnp.max(jnp.where(to_home & my_later, blocks, 0), axis=1)
    to_plane = my_plane[None, :] == ((my_z + steps) % Z)[:, None]
    second_blocks = jnp.max(jnp.where(to_plane & my_later, blocks, 0), axis=1)

    main_send, *second_send = send_tiles(main_blocks, second_blocks, gen_mat, ham_mat)
    second_send[0], owner_late = lax.optimization_barrier((second_send[0], owner_all))
    rank_all, double_all = homes_of(owner_late)
    planes_all = ((rank_all % Z)[..., None] == steps).astype(BF16)
    in_plane = jnp.einsum("gck,gkt->gct", double_all.astype(BF16), planes_all, preferred_element_type=F32)
    crowded = jnp.max(in_plane) > 1.5

    shifted = [z_shift(second_send[s], s) for s in range(1, Z)]
    main = exchanged(main_send)
    ladder = ladder_term(gen_mat, ham_mat, occ_row)

    second_z = jnp.stack([second_send[0]] + shifted)
    same = [second_z] + [x_shift(second_z, s, 0) for s in range(1, X)]
    seconds = same + [x_shift(part, 0, 1) for part in same]

    here = dest == me
    main_place = jnp.max(jnp.where(here & ~later, offsets, -1), axis=1)
    second_place = jnp.max(jnp.where(here & later, offsets, -1), axis=1)
    flips = jnp.arange(CORE, dtype=jnp.int32)[:, None]
    shifts = jnp.arange(X, dtype=jnp.int32)[None, :]
    from_z = (my_z - steps) % Z
    came_from = chan_of(((my_x - shifts) % X)[..., None], from_z, (my_core ^ flips)[..., None]).reshape(-1)
    place_in = jnp.sum(jnp.where(came_from[:, None] == names, second_place, 0), axis=1)

    mirror = [(g, g ^ 1) for g in range(lax.axis_size("grp"))]
    slots = jnp.where(my_later, -1, my_dest)
    own_planes = jnp.where(my_later, my_plane, -1)

    def of_partner(array):
        return lax.dynamic_index_in_dim(array, grp ^ 1, 0, keepdims=False)

    named = lax.dynamic_index_in_dim(of_partner(owner_late), me, 0, keepdims=False)
    named_one = (named[:, None] == names).astype(BF16)
    named_plane = jnp.dot(named_one, of_partner(planes_all), preferred_element_type=F32)
    named_plane = jnp.sum(named_plane.astype(jnp.int32) * steps, axis=-1)
    named_later = jnp.any((named[None, :] == named[:, None]) & (blocks[None, :] < blocks[:, None]), axis=-1)
    partner_planes = jnp.where(named_later, named_plane, -1)

    main, ladder, crowded, slots, own_planes, partner_planes = lax.optimization_barrier(
        (main, ladder, crowded, slots, own_planes, partner_planes)
    )
    gen_full, ham_full = placed(main_place, place_in, main, seconds)
    cross = pair_product(gen_full, ham_full, ham_full, gen_full)
    back_main_offsets = jnp.maximum(main_place, 0)

    piece_of = (((my_x + shifts) % X) * CORE + (my_core ^ flips)).reshape(-1)
    upper_send, lower_rows, *pieces = back_tiles(back_main_offsets, second_place, piece_of, cross)
    upper = exchanged(upper_send)
    routed = [
        x_shift(piece, step, flip) if step or flip else piece
        for (step, flip), piece in zip(RELATIVE, pieces)
    ]
    in_my_plane = later & ((dest // CORE) % Z == my_z)
    holder = jnp.max(jnp.where(in_my_plane, dest, 0), axis=1)
    choice = ((holder % CORE) ^ my_core) * X + (my_x - holder // (Z * CORE)) % X
    lower_send = joined(choice, lower_rows, routed)
    lower = exchanged(lower_send)

    upper_own = gathered(slots, upper)
    upper_partner = lax.ppermute(upper_own, "grp", mirror)
    lower_own = gathered_lower(slots, jnp.maximum(own_planes, 0), lower)
    lower_partner = lax.ppermute(lower_own, "grp", mirror)

    def fast():
        own, partner = (upper_own, lower_own), (upper_partner, lower_partner)
        return assembled(own_planes, partner_planes, ladder, own, partner)

    def slow():
        arrived = exchanged(direct_tiles(direct_blocks, gen_mat, ham_mat))
        gen_slow, ham_slow = placed(main_place, second_place, main, [arrived])
        cross_slow = commutator_by_rows(gen_slow, ham_slow)
        back = exchanged(back_direct(back_main_offsets, jnp.maximum(second_place, 0), cross_slow))
        back = back.reshape(2 * CHAN, TILE, TILE)
        own = gathered(2 * my_dest + my_later.astype(jnp.int32), back)
        partner = in_bands(lax.ppermute(own, "grp", mirror))
        nowhere = jnp.full((BLOCKS,), -1, jnp.int32)
        return assembled(nowhere, nowhere, ladder, in_bands(own), partner)

    return lax.cond(crowded, slow, fast)[None, None]


def solution(mesh):
    in_specs = (
        P("grp", "chan", None, None),
        P("grp", "chan", None, None),
        P("grp", "chan", None),
        P(),
        P(),
    )
    out_specs = P("grp", "chan", None, None)

    return jax.shard_map(
        on_device, mesh=mesh, in_specs=in_specs, out_specs=out_specs, check_vma=False
    )
```

profile of v0, /device:TPU:1, one launch (start us, length us, event | category | flops | bytes accessed | tf_op | source)
XLA Modules:
  0.0 297.1 jit_solution(10612549862709018132)
XLA Ops:
  1.6 1.6 select_reduce_fusion.1
  4.5 4.1 %shard_map.57 = (bf16[64,2,128,128]{3,2,1,0:T(8,128)(2,1)S(1)}, bf16[2,128,128]{2,1,0:T(8,128)(2,1)S(1)}, bf16[2,128,128]{2,1,0:T(8,128)(2,1)S(1)}, bf16[2,128,1...) custom-call(s32[64]{0:T(128)S(1)} %select_reduce_fusion.4.main_table, ...), custom_call_target="tpu_custom_call" | custom-call | tf_op jit(solution)/shard_map/pallas_call | solution.py:54
  8.7 2.0 copy-done.4
  10.6 13.3 %all-to-all-start.2 = ((bf16[64,2,128,128]{3,2,1,0:T(8,128)(2,1)}), bf16[64,2,128,128]{3,2,1,0:T(8,128)(2,1)}, u32[]{:S(2)}, u32[]{:S(2)}) async-start(bf16[64,2,128,128]{3,2,1,0:T(8,128)(2,1)} %copy-done.4), calls=%async_computation.2 | async-start | bytes 8388608 | tf_op jit(solution)/shard_map/all_to_all | solution.py:50
  23.9 1.4 collective-permute-start.1
  25.3 2.1 collective-permute-start.2
  27.4 2.4 collective-permute-start.3
  29.8 2.1 collective-permute-start.4
  31.9 2.4 collective-permute-start.5
  35.9 2.3 convert_reduce_fusion
  40.5 76.1 %collective-permute-done.1 = bf16[2,128,128]{2,1,0:T(8,128)(2,1)S(1)} collective-permute-done((bf16[2,128,128]{2,1,0:T(8,128)(2,1)S(1)}, bf16[2,128,128]{2,1,0:T(8,128)(2,1)S(1)}, u32[]{:S(2)}, u32[]{:S(2)}) %collective-permute-start.1) | collective-permute-done | bytes 65568 | tf_op jit(solution)/shard_map/ppermute | solution.py:36
  116.7 2.0 collective-permute-start.6
  118.7 2.4 collective-permute-done.2
  121.8 2.1 collective-permute-done.3
  123.9 5.1 %collective-permute-done.4 = bf16[2,128,128]{2,1,0:T(8,128)(2,1)S(1)} collective-permute-done((bf16[2,128,128]{2,1,0:T(8,128)(2,1)S(1)}, bf16[2,128,128]{2,1,0:T(8,128)(2,1)S(1)}, u32[]{:S(2)}, u32[]{:S(2)}) %collective-permute-start.4) | collective-permute-done | bytes 65568 | tf_op jit(solution)/shard_map/ppermute | solution.py:36
  129.2 1.3 collective-permute-start.8
  130.5 2.6 collective-permute-start.9
  133.1 1.1 collective-permute-start.10
  134.4 4.0 %fusion.1 = f32[896,896]{1,0:T(8,128)S(1)} fusion(bf16[1,1,896,896]{3,2,1,0:T(8,128)(2,1)} %param.7, f32[896]{0:T(1024)S(1)} %reduce.4, bf16[1,1,896,896]{3,2,1,0:T(8,128)(2,1)} %param.8), kind=kOutput, calls=%fused_computation.10 | convolution fusion | flops 1441054720 | bytes 6426112 | tf_op jit(solution)/shard_map/dot_general | solution.py:307
  138.4 3.4 %collective-permute-start.11 = (bf16[8,2,128,128]{3,2,1,0:T(8,128)(2,1)S(1)}, bf16[8,2,128,128]{3,2,1,0:T(8,128)(2,1)S(1)}, u32[]{:S(2)}, u32[]{:S(2)}) collective-permute-start(bf16[8,2,128,128]{3,2,1,0:T(8,128)(2,1)S(1)} %bitcast_dynamic-update-slice_fusion.refs_0_), channel_id=1, source_target_pairs={{0,1},{1,0},{2,3},{3,2},{4,5},{5,4},{6,7},{7,6},{8,9},{9,8},{10,11... | collective-permute-start | bytes 1572872 | tf_op jit(solution)/shard_map/ppermute | solution.py:46
  141.9 4.7 %collective-permute-start.12 = (bf16[8,2,128,128]{3,2,1,0:T(8,128)(2,1)S(1)}, bf16[8,2,128,128]{3,2,1,0:T(8,128)(2,1)S(1)}, u32[]{:S(2)}, u32[]{:S(2)}) collective-permute-start(bf16[8,2,128,128]{3,2,1,0:T(8,128)(2,1)S(1)} %collective-permute-done.8.refs_1_), channel_id=1, source_target_pairs={{0,1},{1,0},{2,3},{3,2},{4,5},{5,4},{6,7},{7,6},{8,9},{9,8},{10,11... | collective-permute-start | bytes 1572872 | tf_op jit(solution)/shard_map/ppermute | solution.py:46
  146.6 7.2 %collective-permute-done.9.refs_2_ = bf16[8,2,128,128]{3,2,1,0:T(8,128)(2,1)S(1)} collective-permute-done((bf16[8,2,128,128]{3,2,1,0:T(8,128)(2,1)S(1)}, bf16[8,2,128,128]{3,2,1,0:T(8,128)(2,1)S(1)}, u32[]{:S(2)}, u32[]{:S(2)}) %collective-permute-start.9) | collective-permute-done | bytes 524320 | tf_op jit(solution)/shard_map/ppermute | solution.py:46
  153.8 3.4 %collective-permute-start.13 = (bf16[8,2,128,128]{3,2,1,0:T(8,128)(2,1)S(1)}, bf16[8,2,128,128]{3,2,1,0:T(8,128)(2,1)}, u32[]{:S(2)}, u32[]{:S(2)}) collective-permute-start(bf16[8,2,128,128]{3,2,1,0:T(8,128)(2,1)S(1)} %collective-permute-done.9.refs_2_), channel_id=1, source_target_pairs={{0,1},{1,0},{2,3},{3,2},{4,5},{5,4},{6,7},{7,6},{8,9},{9,8},{10,11... | collective-permute-start | bytes 1572872 | tf_op jit(solution)/shard_map/ppermute | solution.py:46
  157.2 3.7 %convolution_subtract_fusion.1 = f32[896,896]{1,0:T(8,128)} fusion(f32[896,896]{1,0:T(8,128)S(1)} %fusion.1, bf16[1,1,896,896]{3,2,1,0:T(8,128)(2,1)S(1)} %copy-done.11, f32[896]{0:T(1024)S(1)} %reduce.4, bf16[1,1,896,896]{3,2,1,0:T(8,128)(2,1)S(1)} %copy-done.10), kind=kOutput, calls=%fused_computation.8 | convolution fusion | flops 1441857536 | bytes 9637376 | tf_op jit(solution)/shard_map/dot_general | solution.py:308
  161.0 6.2 %shard_map.58 = (bf16[896,896]{1,0:T(8,128)(2,1)S(1)}, bf16[896,896]{1,0:T(8,128)(2,1)S(1)}) custom-call(s32[64]{0:T(128)S(1)} %get-tuple-element.162.main_table, s32[64]{0:T(128)S(1)} %select_reduce_fusion.2.second_table, bf16[64,2,128,128]{3,2,1,0:T(8,128)(2,1)} %all-to-all-done.2.main_ref, ...), custom_call_target="tpu_custom_call" | custom-call | tf_op jit(solution)/shard_map/pallas_call | solution.py:54
  167.2 2.0 fusion.41
  169.2 2.0 convolution_subtract_fusion.cross_ref
  171.2 2.5 shard_map.59
  173.8 1.2 copy-done.5
  177.1 7.3 %all-to-all-start.3 = ((bf16[64,112,128]{2,1,0:T(8,128)(2,1)}), bf16[64,112,128]{2,1,0:T(8,128)(2,1)S(1)}, u32[]{:S(2)}, u32[]{:S(2)}) async-start(bf16[64,112,128]{2,1,0:T(8,128)(2,1)} %copy-done.5), calls=%async_computation.3 | async-start | bytes 3670016 | tf_op jit(solution)/shard_map/all_to_all | solution.py:50
  184.4 1.4 collective-permute-start.15
  185.9 2.6 collective-permute-start.16
  188.5 1.1 collective-permute-start.17
  189.5 1.2 collective-permute-start.18
  191.0 8.3 %collective-permute-done.15.refs_1_ = bf16[64,16,128]{2,1,0:T(8,128)(2,1)S(1)} collective-permute-done((bf16[64,16,128]{2,1,0:T(8,128)(2,1)}, bf16[64,16,128]{2,1,0:T(8,128)(2,1)S(1)}, u32[]{:S(2)}, u32[]{:S(2)}) %collective-permute-start.15) | collective-permute-done | bytes 262176 | tf_op jit(solution)/shard_map/ppermute | solution.py:46
  199.3 12.4 %collective-permute-start.20 = (bf16[64,16,128]{2,1,0:T(8,128)(2,1)S(1)}, bf16[64,16,128]{2,1,0:T(8,128)(2,1)S(1)}, u32[]{:S(2)}, u32[]{:S(2)}) collective-permute-start(bf16[64,16,128]{2,1,0:T(8,128)(2,1)S(1)} %get-tuple-element.134), channel_id=1, source_target_pairs={{0,33},{1,32},{2,35},{3,34},{4,37},{5,36},{6,39},{7,38},{8,41},{9,... | collective-permute-start | bytes 786440 | tf_op jit(solution)/shard_map/ppermute | solution.py:46
  211.8 10.1 %collective-permute-done.19.refs_5_ = bf16[64,16,128]{2,1,0:T(8,128)(2,1)S(1)} collective-permute-done((bf16[64,16,128]{2,1,0:T(8,128)(2,1)S(1)}, bf16[64,16,128]{2,1,0:T(8,128)(2,1)S(1)}, u32[]{:S(2)}, u32[]{:S(2)}) %collective-permute-start.19) | collective-permute-done | bytes 262176 | tf_op jit(solution)/shard_map/ppermute | solution.py:46
  222.0 8.5 %collective-permute-done.20.refs_6_ = bf16[64,16,128]{2,1,0:T(8,128)(2,1)S(1)} collective-permute-done((bf16[64,16,128]{2,1,0:T(8,128)(2,1)S(1)}, bf16[64,16,128]{2,1,0:T(8,128)(2,1)S(1)}, u32[]{:S(2)}, u32[]{:S(2)}) %collective-permute-start.20) | collective-permute-done | bytes 262176 | tf_op jit(solution)/shard_map/ppermute | solution.py:46
  230.5 4.5 %shard_map.61 = bf16[64,32,128]{2,1,0:T(8,128)(2,1)} custom-call(s32[64]{0:T(128)S(1)} %fusion.30.table, bf16[64,16,128]{2,1,0:T(8,128)(2,1)S(1)} %get-tuple-element.127.lower_ref, bf16[64,16,128]{2,1,0:T(8,128)(2,1)S(1)} %get-tuple-element.128.refs_0_, bf16[64,16,128]{2,1,0:T(8,128)(2,1)S(1)} %collective-permute-done.15.refs_1_, ...), custom_call_target="tpu_custom_call" | custom-call | tf_op jit(solution)/shard_map/pallas_call | solution.py:54
  235.0 9.6 %all-to-all-start.4 = ((bf16[64,32,128]{2,1,0:T(8,128)(2,1)}), bf16[64,32,128]{2,1,0:T(8,128)(2,1)S(1)}, u32[]{:S(2)}, u32[]{:S(2)}) async-start(bf16[64,32,128]{2,1,0:T(8,128)(2,1)} %shard_map.61), calls=%async_computation.4 | async-start | bytes 1048576 | tf_op jit(solution)/shard_map/all_to_all | solution.py:50
  244.6 2.3 shard_map.60
  246.9 1.3 collective-permute-start.22
  248.2 13.6 %all-to-all-done.4.main_ref = bf16[64,32,128]{2,1,0:T(8,128)(2,1)S(1)} async-done(((bf16[64,32,128]{2,1,0:T(8,128)(2,1)}), bf16[64,32,128]{2,1,0:T(8,128)(2,1)S(1)}, u32[]{:S(2)}, u32[]{:S(2)}) %all-to-all-start.4) | async-done | bytes 524320 | tf_op jit(solution)/shard_map/all_to_all | solution.py:50
  261.9 1.5 shard_map.62
  263.4 1.4 collective-permute-start.23
  264.8 23.4 %collective-permute-done.23 = bf16[105,16,128]{2,1,0:T(8,128)(2,1)S(1)} collective-permute-done((bf16[105,16,128]{2,1,0:T(8,128)(2,1)S(1)}, bf16[105,16,128]{2,1,0:T(8,128)(2,1)S(1)}, u32[]{:S(2)}, u32[]{:S(2)}) %collective-permute-start.23) | collective-permute-done | bytes 430112 | tf_op jit(solution)/shard_map/ppermute | solution.py:435
  288.3 7.9 %conditional.1 = (f32[1,1,896,896]{3,2,1,0:T(8,128)}) conditional(s32[]{:T(128)} %convert_element_type.63, (s32[49]{0:T(128)S(1)}, s32[49]{0:T(128)S(1)}, f32[896,896]{1,0:T(8,128)}, bf16[49,112,128]{2,1,0:T(8,128)(2,1)}, bf16[105,16,128]{2,1,0:T(8,128)(2,1)S(1)}, /*index=5*/bf16[49,112,128]{2,1,0:T(8,128)(2,1)S(1)}, ...), branch_computations={%region_17.18_spmd, %region_18.20_spmd} | conditional | flops 9555 | bytes 78049072 | solution.py:452
  288.3 7.9 %branch_0_fun.1 = f32[896,896]{1,0:T(8,128)} custom-call(s32[49]{0:T(128)S(1)} %get-tuple-element.53.own_table, s32[49]{0:T(128)S(1)} %get-tuple-element.54.partner_table, f32[896,896]{1,0:T(8,128)} %get-tuple-element.55.ladder_ref, bf16[49,112,128]{2,1,0:T(8,128)(2,1)} %get-tuple-element.56.upper, bf16[105,16,128]{2,1,0:T(8,128)(2,1)S(1)} %get-tuple-element.57.lower, ...), custom_call_target="tpu_custom_call" | custom-call | tf_op jit(solution)/shard_map/cond/branch_0_fun/pallas_call | solution.py:290
  (91 shorter events, 10.4 us)
Async XLA Ops:
  0.0 35.9 %copy-start = (s32[4,64,49]{1,0,2:T(4,128)S(1)}, s32[4,64,49]{1,0,2:T(4,128)}, u32[]{:S(2)}) copy-start(s32[4,64,49]{1,0,2:T(4,128)} %param.11) | copy-start | bytes 150532
  8.6 2.0 copy-start.4
  10.6 23.7 %copy-start.12 = (s32[4,64,49,1]{1,3,2,0:T(1,128)S(1)}, s32[4,64,49,1]{1,3,2,0:T(1,128)}, u32[]{:S(2)}) copy-start(s32[4,64,49,1]{1,3,2,0:T(1,128)} %param.10) | copy-start | bytes 150532
  10.6 29.9 %copy-start.13 = (f32[1,1,896]{2,1,0:T(1,128)S(1)}, f32[1,1,896]{2,1,0:T(1,128)}, u32[]{:S(2)}) copy-start(f32[1,1,896]{2,1,0:T(1,128)} %param.9) | copy-start | bytes 10756
  10.6 150.3 %all-to-all-start.2 = ((bf16[64,2,128,128]{3,2,1,0:T(8,128)(2,1)}), bf16[64,2,128,128]{3,2,1,0:T(8,128)(2,1)}, u32[]{:S(2)}, u32[]{:S(2)}) async-start(bf16[64,2,128,128]{3,2,1,0:T(8,128)(2,1)} %copy-done.4), calls=%async_computation.2 | async-start | bytes 8388608 | tf_op jit(solution)/shard_map/all_to_all | solution.py:50
  23.9 92.7 %collective-permute-start.1 = (bf16[2,128,128]{2,1,0:T(8,128)(2,1)S(1)}, bf16[2,128,128]{2,1,0:T(8,128)(2,1)S(1)}, u32[]{:S(2)}, u32[]{:S(2)}) collective-permute-start(bf16[2,128,128]{2,1,0:T(8,128)(2,1)S(1)} %get-tuple-element.117), channel_id=1, source_target_pairs={{0,2},{1,3},{2,4},{3,5},{4,6},{5,7},{6,8},{7,9},{8,10},{9,11},{10,... | collective-permute-start | bytes 196616 | tf_op jit(solution)/shard_map/ppermute | solution.py:36
  25.3 95.7 %collective-permute-start.2 = (bf16[2,128,128]{2,1,0:T(8,128)(2,1)S(1)}, bf16[2,128,128]{2,1,0:T(8,128)(2,1)S(1)}, u32[]{:S(2)}, u32[]{:S(2)}) collective-permute-start(bf16[2,128,128]{2,1,0:T(8,128)(2,1)S(1)} %get-tuple-element.118), channel_id=1, source_target_pairs={{0,4},{1,5},{2,6},{3,7},{4,8},{5,9},{6,10},{7,11},{8,12},{9,13},{1... | collective-permute-start | bytes 196616 | tf_op jit(solution)/shard_map/ppermute | solution.py:36
  27.4 96.5 %collective-permute-start.3 = (bf16[2,128,128]{2,1,0:T(8,128)(2,1)S(1)}, bf16[2,128,128]{2,1,0:T(8,128)(2,1)S(1)}, u32[]{:S(2)}, u32[]{:S(2)}) collective-permute-start(bf16[2,128,128]{2,1,0:T(8,128)(2,1)S(1)} %get-tuple-element.119), channel_id=1, source_target_pairs={{0,6},{1,7},{2,8},{3,9},{4,10},{5,11},{6,12},{7,13},{8,14},{9,15},... | collective-permute-start | bytes 196616 | tf_op jit(solution)/shard_map/ppermute | solution.py:36
  29.8 99.2 %collective-permute-start.4 = (bf16[2,128,128]{2,1,0:T(8,128)(2,1)S(1)}, bf16[2,128,128]{2,1,0:T(8,128)(2,1)S(1)}, u32[]{:S(2)}, u32[]{:S(2)}) collective-permute-start(bf16[2,128,128]{2,1,0:T(8,128)(2,1)S(1)} %get-tuple-element.120), channel_id=1, source_target_pairs={{0,8},{1,9},{2,10},{3,11},{4,12},{5,13},{6,14},{7,15},{8,0},{9,1},... | collective-permute-start | bytes 196616 | tf_op jit(solution)/shard_map/ppermute | solution.py:36
  31.9 97.2 %collective-permute-start.5 = (bf16[2,128,128]{2,1,0:T(8,128)(2,1)S(1)}, bf16[2,128,128]{2,1,0:T(8,128)(2,1)S(1)}, u32[]{:S(2)}, u32[]{:S(2)}) collective-permute-start(bf16[2,128,128]{2,1,0:T(8,128)(2,1)S(1)} %get-tuple-element.121), channel_id=1, source_target_pairs={{0,10},{1,11},{2,12},{3,13},{4,14},{5,15},{6,0},{7,1},{8,2},{9,3},... | collective-permute-start | bytes 196616 | tf_op jit(solution)/shard_map/ppermute | solution.py:36
  116.7 12.5 %collective-permute-start.6 = (bf16[2,128,128]{2,1,0:T(8,128)(2,1)S(1)}, bf16[2,128,128]{2,1,0:T(8,128)(2,1)S(1)}, u32[]{:S(2)}, u32[]{:S(2)}) collective-permute-start(bf16[2,128,128]{2,1,0:T(8,128)(2,1)S(1)} %get-tuple-element.122), channel_id=1, source_target_pairs={{0,12},{1,13},{2,14},{3,15},{4,0},{5,1},{6,2},{7,3},{8,4},{9,5},{1... | collective-permute-start | bytes 196616 | tf_op jit(solution)/shard_map/ppermute | solution.py:36
  121.0 8.1 %collective-permute-start.7 = (bf16[2,128,128]{2,1,0:T(8,128)(2,1)S(1)}, bf16[2,128,128]{2,1,0:T(8,128)(2,1)S(1)}, u32[]{:S(2)}, u32[]{:S(2)}) collective-permute-start(bf16[2,128,128]{2,1,0:T(8,128)(2,1)S(1)} %get-tuple-element.123), channel_id=1, source_target_pairs={{0,14},{1,15},{2,0},{3,1},{4,2},{5,3},{6,4},{7,5},{8,6},{9,7},{10,... | collective-permute-start | bytes 196616 | tf_op jit(solution)/shard_map/ppermute | solution.py:36
  129.2 12.7 %collective-permute-start.8 = (bf16[8,2,128,128]{3,2,1,0:T(8,128)(2,1)S(1)}, bf16[8,2,128,128]{3,2,1,0:T(8,128)(2,1)S(1)}, u32[]{:S(2)}, u32[]{:S(2)}) collective-permute-start(bf16[8,2,128,128]{3,2,1,0:T(8,128)(2,1)S(1)} %bitcast_dynamic-update-slice_fusion.refs_0_), channel_id=1, source_target_pairs={{0,16},{1,17},{2,18},{3,19},{4,20},{5,21},{6,22},{7,23},{8,24},{9,... | collective-permute-start | bytes 1572872 | tf_op jit(solution)/shard_map/ppermute | solution.py:46
  130.5 23.3 %collective-permute-start.9 = (bf16[8,2,128,128]{3,2,1,0:T(8,128)(2,1)S(1)}, bf16[8,2,128,128]{3,2,1,0:T(8,128)(2,1)S(1)}, u32[]{:S(2)}, u32[]{:S(2)}) collective-permute-start(bf16[8,2,128,128]{3,2,1,0:T(8,128)(2,1)S(1)} %bitcast_dynamic-update-slice_fusion.refs_0_), channel_id=1, source_target_pairs={{0,32},{1,33},{2,34},{3,35},{4,36},{5,37},{6,38},{7,39},{8,40},{9,... | collective-permute-start | bytes 1572872 | tf_op jit(solution)/shard_map/ppermute | solution.py:46
  133.1 24.1 %collective-permute-start.10 = (bf16[8,2,128,128]{3,2,1,0:T(8,128)(2,1)S(1)}, bf16[8,2,128,128]{3,2,1,0:T(8,128)(2,1)S(1)}, u32[]{:S(2)}, u32[]{:S(2)}) collective-permute-start(bf16[8,2,128,128]{3,2,1,0:T(8,128)(2,1)S(1)} %bitcast_dynamic-update-slice_fusion.refs_0_), channel_id=1, source_target_pairs={{0,48},{1,49},{2,50},{3,51},{4,52},{5,53},{6,54},{7,55},{8,56},{9,... | collective-permute-start | bytes 1572872 | tf_op jit(solution)/shard_map/ppermute | solution.py:46
  134.3 22.9 %copy-start.10 = (bf16[1,1,896,896]{3,2,1,0:T(8,128)(2,1)S(1)}, bf16[1,1,896,896]{3,2,1,0:T(8,128)(2,1)}, u32[]{:S(2)}) copy-start(bf16[1,1,896,896]{3,2,1,0:T(8,128)(2,1)} %param.7) | copy-start | bytes 4816900
  134.4 22.9 %copy-start.11 = (bf16[1,1,896,896]{3,2,1,0:T(8,128)(2,1)S(1)}, bf16[1,1,896,896]{3,2,1,0:T(8,128)(2,1)}, u32[]{:S(2)}) copy-start(bf16[1,1,896,896]{3,2,1,0:T(8,128)(2,1)} %param.8) | copy-start | bytes 4816900
  138.4 22.5 %collective-permute-start.11 = (bf16[8,2,128,128]{3,2,1,0:T(8,128)(2,1)S(1)}, bf16[8,2,128,128]{3,2,1,0:T(8,128)(2,1)S(1)}, u32[]{:S(2)}, u32[]{:S(2)}) collective-permute-start(bf16[8,2,128,128]{3,2,1,0:T(8,128)(2,1)S(1)} %bitcast_dynamic-update-slice_fusion.refs_0_), channel_id=1, source_target_pairs={{0,1},{1,0},{2,3},{3,2},{4,5},{5,4},{6,7},{7,6},{8,9},{9,8},{10,11... | collective-permute-start | bytes 1572872 | tf_op jit(solution)/shard_map/ppermute | solution.py:46
  141.9 19.1 %collective-permute-start.12 = (bf16[8,2,128,128]{3,2,1,0:T(8,128)(2,1)S(1)}, bf16[8,2,128,128]{3,2,1,0:T(8,128)(2,1)S(1)}, u32[]{:S(2)}, u32[]{:S(2)}) collective-permute-start(bf16[8,2,128,128]{3,2,1,0:T(8,128)(2,1)S(1)} %collective-permute-done.8.refs_1_), channel_id=1, source_target_pairs={{0,1},{1,0},{2,3},{3,2},{4,5},{5,4},{6,7},{7,6},{8,9},{9,8},{10,11... | collective-permute-start | bytes 1572872 | tf_op jit(solution)/shard_map/ppermute | solution.py:46
  153.8 7.1 %collective-permute-start.13 = (bf16[8,2,128,128]{3,2,1,0:T(8,128)(2,1)S(1)}, bf16[8,2,128,128]{3,2,1,0:T(8,128)(2,1)}, u32[]{:S(2)}, u32[]{:S(2)}) collective-permute-start(bf16[8,2,128,128]{3,2,1,0:T(8,128)(2,1)S(1)} %collective-permute-done.9.refs_2_), channel_id=1, source_target_pairs={{0,1},{1,0},{2,3},{3,2},{4,5},{5,4},{6,7},{7,6},{8,9},{9,8},{10,11... | collective-permute-start | bytes 1572872 | tf_op jit(solution)/shard_map/ppermute | solution.py:46
  157.2 3.8 %collective-permute-start.14 = (bf16[8,2,128,128]{3,2,1,0:T(8,128)(2,1)S(1)}, bf16[8,2,128,128]{3,2,1,0:T(8,128)(2,1)}, u32[]{:S(2)}, u32[]{:S(2)}) collective-permute-start(bf16[8,2,128,128]{3,2,1,0:T(8,128)(2,1)S(1)} %collective-permute-done.10.refs_3_), channel_id=1, source_target_pairs={{0,1},{1,0},{2,3},{3,2},{4,5},{5,4},{6,7},{7,6},{8,9},{9,8},{10,11... | collective-permute-start | bytes 1572872 | tf_op jit(solution)/shard_map/ppermute | solution.py:46
  173.8 1.2 copy-start.5
  175.0 0.7 copy-start.6
  175.7 0.7 copy-start.7
  176.4 0.7 copy-start.8
  177.1 57.9 %all-to-all-start.3 = ((bf16[64,112,128]{2,1,0:T(8,128)(2,1)}), bf16[64,112,128]{2,1,0:T(8,128)(2,1)S(1)}, u32[]{:S(2)}, u32[]{:S(2)}) async-start(bf16[64,112,128]{2,1,0:T(8,128)(2,1)} %copy-done.5), calls=%async_computation.3 | async-start | bytes 3670016 | tf_op jit(solution)/shard_map/all_to_all | solution.py:50
  184.4 14.9 %collective-permute-start.15 = (bf16[64,16,128]{2,1,0:T(8,128)(2,1)}, bf16[64,16,128]{2,1,0:T(8,128)(2,1)S(1)}, u32[]{:S(2)}, u32[]{:S(2)}) collective-permute-start(bf16[64,16,128]{2,1,0:T(8,128)(2,1)} %copy-done.8), channel_id=1, source_target_pairs={{0,16},{1,17},{2,18},{3,19},{4,20},{5,21},{6,22},{7,23},{8,24},{9,... | collective-permute-start | bytes 786440 | tf_op jit(solution)/shard_map/ppermute | solution.py:46
  185.9 25.9 %collective-permute-start.16 = (bf16[64,16,128]{2,1,0:T(8,128)(2,1)}, bf16[64,16,128]{2,1,0:T(8,128)(2,1)S(1)}, u32[]{:S(2)}, u32[]{:S(2)}) collective-permute-start(bf16[64,16,128]{2,1,0:T(8,128)(2,1)} %copy-done.7), channel_id=1, source_target_pairs={{0,32},{1,33},{2,34},{3,35},{4,36},{5,37},{6,38},{7,39},{8,40},{9,... | collective-permute-start | bytes 786440 | tf_op jit(solution)/shard_map/ppermute | solution.py:46
  188.5 23.3 %collective-permute-start.17 = (bf16[64,16,128]{2,1,0:T(8,128)(2,1)}, bf16[64,16,128]{2,1,0:T(8,128)(2,1)S(1)}, u32[]{:S(2)}, u32[]{:S(2)}) collective-permute-start(bf16[64,16,128]{2,1,0:T(8,128)(2,1)} %copy-done.6), channel_id=1, source_target_pairs={{0,48},{1,49},{2,50},{3,51},{4,52},{5,53},{6,54},{7,55},{8,56},{9,... | collective-permute-start | bytes 786440 | tf_op jit(solution)/shard_map/ppermute | solution.py:46
  189.5 22.3 %collective-permute-start.18 = (bf16[64,16,128]{2,1,0:T(8,128)(2,1)S(1)}, bf16[64,16,128]{2,1,0:T(8,128)(2,1)S(1)}, u32[]{:S(2)}, u32[]{:S(2)}) collective-permute-start(bf16[64,16,128]{2,1,0:T(8,128)(2,1)S(1)} %get-tuple-element.132), channel_id=1, source_target_pairs={{0,1},{1,0},{2,3},{3,2},{4,5},{5,4},{6,7},{7,6},{8,9},{9,8},{10,11... | collective-permute-start | bytes 786440 | tf_op jit(solution)/shard_map/ppermute | solution.py:46
  190.8 31.2 %collective-permute-start.19 = (bf16[64,16,128]{2,1,0:T(8,128)(2,1)S(1)}, bf16[64,16,128]{2,1,0:T(8,128)(2,1)S(1)}, u32[]{:S(2)}, u32[]{:S(2)}) collective-permute-start(bf16[64,16,128]{2,1,0:T(8,128)(2,1)S(1)} %get-tuple-element.133), channel_id=1, source_target_pairs={{0,17},{1,16},{2,19},{3,18},{4,21},{5,20},{6,23},{7,22},{8,25},{9,... | collective-permute-start | bytes 786440 | tf_op jit(solution)/shard_map/ppermute | solution.py:46
  199.3 31.2 %collective-permute-start.20 = (bf16[64,16,128]{2,1,0:T(8,128)(2,1)S(1)}, bf16[64,16,128]{2,1,0:T(8,128)(2,1)S(1)}, u32[]{:S(2)}, u32[]{:S(2)}) collective-permute-start(bf16[64,16,128]{2,1,0:T(8,128)(2,1)S(1)} %get-tuple-element.134), channel_id=1, source_target_pairs={{0,33},{1,32},{2,35},{3,34},{4,37},{5,36},{6,39},{7,38},{8,41},{9,... | collective-permute-start | bytes 786440 | tf_op jit(solution)/shard_map/ppermute | solution.py:46
  211.8 18.7 %collective-permute-start.21 = (bf16[64,16,128]{2,1,0:T(8,128)(2,1)S(1)}, bf16[64,16,128]{2,1,0:T(8,128)(2,1)S(1)}, u32[]{:S(2)}, u32[]{:S(2)}) collective-permute-start(bf16[64,16,128]{2,1,0:T(8,128)(2,1)S(1)} %get-tuple-element.135), channel_id=1, source_target_pairs={{0,49},{1,48},{2,51},{3,50},{4,53},{5,52},{6,55},{7,54},{8,57},{9,... | collective-permute-start | bytes 786440 | tf_op jit(solution)/shard_map/ppermute | solution.py:46
  235.0 26.9 %all-to-all-start.4 = ((bf16[64,32,128]{2,1,0:T(8,128)(2,1)}), bf16[64,32,128]{2,1,0:T(8,128)(2,1)S(1)}, u32[]{:S(2)}, u32[]{:S(2)}) async-start(bf16[64,32,128]{2,1,0:T(8,128)(2,1)} %shard_map.61), calls=%async_computation.4 | async-start | bytes 1048576 | tf_op jit(solution)/shard_map/all_to_all | solution.py:50
  246.9 41.3 %collective-permute-start.22 = (bf16[49,112,128]{2,1,0:T(8,128)(2,1)}, bf16[49,112,128]{2,1,0:T(8,128)(2,1)S(1)}, u32[]{:S(2)}, u32[]{:S(2)}) collective-permute-start(bf16[49,112,128]{2,1,0:T(8,128)(2,1)} %shard_map.60), channel_id=1, source_target_pairs={{0,64},{64,0},{128,192},{192,128},{1,65},{65,1},{129,193},{193,129... | collective-permute-start | bytes 4214792 | tf_op jit(solution)/shard_map/ppermute | solution.py:433
  263.4 24.9 %collective-permute-start.23 = (bf16[105,16,128]{2,1,0:T(8,128)(2,1)S(1)}, bf16[105,16,128]{2,1,0:T(8,128)(2,1)S(1)}, u32[]{:S(2)}, u32[]{:S(2)}) collective-permute-start(bf16[105,16,128]{2,1,0:T(8,128)(2,1)S(1)} %shard_map.62), channel_id=1, source_target_pairs={{0,64},{64,0},{128,192},{192,128},{1,65},{65,1},{129,193},{193,129... | collective-permute-start | bytes 1290248 | tf_op jit(solution)/shard_map/ppermute | solution.py:435
  296.2 0.9 copy-start.1
where the time goes:
time: 298 us; the launch traced here: 297 us
  waiting for transfers between devices  157 us (53%)
  starting transfers between devices  81.6 us (27%)
  Pallas kernels  29.1 us (10%)
  matrix products  12.8 us (4%)
  local copies, waits for them, and re-layouts  8.35 us (3%)
  other arithmetic  7.11 us (2%)
    ppermute x7, waiting for transfers between devices, z_shift(): return lax.ppermute(value, 'chan', pairs)  85.8 us
    ppermute x14, starting transfers between devices, x_shift(): return lax.ppermute(value, 'chan', pairs)  35.6 us
    ppermute x14, waiting for transfers between devices, x_shift(): return lax.ppermute(value, 'chan', pairs)  34.2 us
    all_to_all x3, starting transfers between devices, exchanged(): lax.all_to_all(value, 'chan', split_axis=0, concat_axis=0, tiled=True)  30.2 us
    ppermute x1, waiting for transfers between devices, on_device(): lower_partner = lax.ppermute(lower_own, 'grp', mirror)  23.4 us
    pallas_call x6, Pallas kernels, kernel_call(): pl.pallas_call(body, out_shape=outs, in_specs=[SMEM] * len(tables) + [VME...  21.2 us
    all_to_all x3, waiting for transfers between devices, exchanged(): lax.all_to_all(value, 'chan', split_axis=0, concat_axis=0, tiled=True)  13.6 us
    ppermute x7, starting transfers between devices, z_shift(): return lax.ppermute(value, 'chan', pairs)  13.1 us
  transfers between devices with their start and end apart: 26, of which 10 were waited for; matrix products, arithmetic and copies ran while one was open for 5% of the time, Pallas kernels for 3%

commit v1 on v0

--- a/solution.py
+++ b/solution.py
@@ -20,6 +20,8 @@
 
 SMEM = pl.BlockSpec(memory_space=pltpu.SMEM)
 VMEM = pl.BlockSpec(memory_space=pltpu.VMEM)
+HBM = pl.BlockSpec(memory_space=pltpu.HBM)
+CHUNKS = 4
 
 
 def chan_of(x, z, core):
@@ -50,14 +52,16 @@
     return lax.all_to_all(value, "chan", split_axis=0, concat_axis=0, tiled=True)
 
 
-def kernel_call(body, tables, arrays, outs, scratch=(), cost=(0, 0)):
+def kernel_call(body, tables, arrays, outs, scratch=(), far_in=0, far_out=0):
+    out_specs = VMEM
+    if isinstance(outs, list):
+        out_specs = [HBM] * far_out + [VMEM] * (len(outs) - far_out)
     return pl.pallas_call(
         body,
         out_shape=outs,
-        in_specs=[SMEM] * len(tables) + [VMEM] * len(arrays),
-        out_specs=jax.tree.map(lambda _: VMEM, outs),
+        in_specs=[SMEM] * len(tables) + [HBM] * far_in + [VMEM] * (len(arrays) - far_in),
+        out_specs=out_specs,
         scratch_shapes=list(scratch),
-        cost_estimate=pl.CostEstimate(flops=cost[0], bytes_accessed=cost[1], transcendentals=0),
         compiler_params=pltpu.CompilerParams(vmem_limit_bytes=LIMIT << 20),
     )(*tables, *arrays)
 
@@ -70,22 +74,33 @@
 
 def send_tiles(main_blocks, second_blocks, gen, ham):
     count = second_blocks.shape[0]
-
-    def body(main_table, second_table, gen_ref, ham_ref, main_ref, *second_refs):
+    chunk = CHAN // CHUNKS
+
+    def body(main_table, second_table, gen_ref, ham_ref, main_ref, *refs):
+        second_refs, (held, done) = refs[:count], refs[count:]
+        copies = []
+        for part in range(CHUNKS):
+
+            @pl.loop(part * chunk, (part + 1) * chunk)
+            def _(slot):
+                block = main_table[slot]
+                held[slot, 0] = tile_at(gen_ref, block)
+                held[slot, 1] = tile_at(ham_ref, block)
+
+            where = pl.ds(part * chunk, chunk)
+            copies.append(pltpu.make_async_copy(held.at[where], main_ref.at[where], done.at[part]))
+            copies[-1].start()
         for step in range(count):
             block = second_table[step]
             second_refs[step][0] = tile_at(gen_ref, block)
             second_refs[step][1] = tile_at(ham_ref, block)
-
-        @pl.loop(0, CHAN)
-        def _(slot):
-            block = main_table[slot]
-            main_ref[slot, 0] = tile_at(gen_ref, block)
-            main_ref[slot, 1] = tile_at(ham_ref, block)
-
-    outs = [jax.ShapeDtypeStruct((CHAN, 2, TILE, TILE), BF16)]
+        for copy in copies:
+            copy.wait()
+
+    outs = [pltpu.HBM((CHAN, 2, TILE, TILE), BF16)]
+    scratch = [pltpu.VMEM(outs[0].shape, BF16), pltpu.SemaphoreType.DMA((CHUNKS,))]
     outs += [jax.ShapeDtypeStruct((2, TILE, TILE), BF16)] * count
-    return kernel_call(body, (main_blocks, second_blocks), (gen, ham), outs)
+    return kernel_call(body, (main_blocks, second_blocks), (gen, ham), outs, scratch, far_out=1)
 
 
 def direct_tiles(blocks, gen, ham):
@@ -103,22 +118,20 @@
 def placed(main_offsets, second_offsets, main, seconds):
     parts = len(seconds)
     each = seconds[0].shape[0]
+    chunk = CHAN // CHUNKS
 
     def body(main_table, second_table, main_ref, *refs):
-        second_refs, (gen_ref, ham_ref, total) = refs[:parts], refs[parts:]
+        second_refs, (gen_ref, ham_ref, total, held, done) = refs[:parts], refs[parts:]
+        copies = []
+        for part in range(CHUNKS):
+            where = pl.ds(part * chunk, chunk)
+            copies.append(pltpu.make_async_copy(main_ref.at[where], held.at[where], done.at[part]))
+            copies[-1].start()
 
         @pl.loop(0, BLOCKS)
         def _(block):
             total[block] = jnp.zeros((2, TILE, TILE), F32)
 
-        @pl.loop(0, CHAN)
-        def _(slot):
-            place = main_table[slot]
-
-            @pl.when(place >= 0)
-            def _():
-                total[place] += main_ref[slot].astype(F32)
-
         for part in range(parts):
 
             @pl.loop(0, each)
@@ -128,6 +141,17 @@
                 @pl.when(place >= 0)
                 def _():
                     total[place] += second_refs[part][slot].astype(F32)
+
+        for part in range(CHUNKS):
+            copies[part].wait()
+
+            @pl.loop(part * chunk, (part + 1) * chunk)
+            def _(slot):
+                place = main_table[slot]
+
+                @pl.when(place >= 0)
+                def _():
+                    total[place] += held[slot].astype(F32)
 
         @pl.loop(0, BLOCKS)
         def _(block):
@@ -137,19 +161,37 @@
             ham_ref[rows, cols] = total[block, 1].astype(BF16)
 
     outs = [jax.ShapeDtypeStruct((SIDE * TILE, SIDE * TILE), BF16)] * 2
-    scratch = [pltpu.VMEM((BLOCKS, 2, TILE, TILE), F32)]
-    return kernel_call(body, (main_offsets, second_offsets), (main, *seconds), outs, scratch)
+    scratch = [
+        pltpu.VMEM((BLOCKS, 2, TILE, TILE), F32),
+        pltpu.VMEM(main.shape, BF16),
+        pltpu.SemaphoreType.DMA((CHUNKS,)),
+    ]
+    tables, arrays = (main_offsets, second_offsets), (main, *seconds)
+    return kernel_call(body, tables, arrays, outs, scratch, far_in=1)
 
 
 def back_tiles(main_offsets, second_offsets, pieces, cross):
     count = len(RELATIVE)
 
-    def body(main_table, second_table, piece_table, cross_ref, upper_ref, lower_ref, *piece_refs):
+    chunk = CHAN // CHUNKS
+
+    def body(main_table, second_table, piece_table, cross_ref, upper_ref, lower_ref, *refs):
+        piece_refs, (held, done) = refs[:count], refs[count:]
+        copies = []
+        for part in range(CHUNKS):
+
+            @pl.loop(part * chunk, (part + 1) * chunk)
+            def _(slot):
+                tile = tile_at(cross_ref, main_table[slot]).astype(BF16)
+                held[slot] = tile[:UPPER]
+                lower_ref[slot] = tile[UPPER:]
+
+            where = pl.ds(part * chunk, chunk)
+            copies.append(pltpu.make_async_copy(held.at[where], upper_ref.at[where], done.at[part]))
+            copies[-1].start()
+
         @pl.loop(0, CHAN)
         def _(slot):
-            tile = tile_at(cross_ref, main_table[slot]).astype(BF16)
-            upper_ref[slot] = tile[:UPPER]
-            lower_ref[slot] = tile[UPPER:]
             block = second_table[slot]
 
             @pl.when(block >= 0)
@@ -161,12 +203,17 @@
                     rows = cross_ref[pl.ds(first, PIECE), pl.ds(col, TILE)]
                     piece_refs[part][slot] = rows.astype(BF16)
 
+        for copy in copies:
+            copy.wait()
+
     outs = [
-        jax.ShapeDtypeStruct((CHAN, UPPER, TILE), BF16),
+        pltpu.HBM((CHAN, UPPER, TILE), BF16),
         jax.ShapeDtypeStruct((CHAN, TILE - UPPER, TILE), BF16),
     ]
+    scratch = [pltpu.VMEM(outs[0].shape, BF16), pltpu.SemaphoreType.DMA((CHUNKS,))]
     outs += [jax.ShapeDtypeStruct((CHAN, PIECE, TILE), BF16)] * count
-    return kernel_call(body, (main_offsets, second_offsets, pieces), (cross,), outs)
+    tables = (main_offsets, second_offsets, pieces)
+    return kernel_call(body, tables, (cross,), outs, scratch, far_out=1)
 
 
 def back_direct(main_offsets, second_offsets, cross):
@@ -181,23 +228,24 @@
 
 
 def joined(choice, lower, routed):
-    rows = TILE - UPPER
+    rows, parts = TILE - UPPER, len(routed)
 
     def body(table, lower_ref, *refs):
-        routed_refs, out_ref = refs[:-1], refs[-1]
+        routed_refs, (out_ref, held) = refs[:parts], refs[parts:]
+
+        @pl.loop(0, CHAN)
+        def _(slot):
+            for part in range(parts):
+                held[part, slot] = routed_refs[part][slot]
 
         @pl.loop(0, CHAN)
         def _(slot):
             out_ref[slot, :rows] = lower_ref[slot]
-            part_of = table[slot]
-            for part, ref in enumerate(routed_refs):
-
-                @pl.when(part_of == part)
-                def _():
-                    out_ref[slot, rows:] = ref[slot]
-
-    out = jax.ShapeDtypeStruct((CHAN, rows + PIECE, TILE), BF16)
-    return kernel_call(body, (choice,), (lower, *routed), out)
+            out_ref[slot, rows:] = held[table[slot], slot]
+
+    out = pltpu.HBM((CHAN, rows + PIECE, TILE), BF16)
+    scratch = [pltpu.VMEM((parts, CHAN, PIECE, TILE), BF16)]
+    return kernel_call(body, (choice,), (lower, *routed), out, scratch)
 
 
 def gathered(slots, main):
@@ -264,43 +312,54 @@
     return kernel_call(body, (slots, planes), (main,), out)
 
 
-def assembled(own_planes, partner_planes, ladder, own, partner):
-    rows = TILE - UPPER
-    units = UPPER // rows
-
-    def tile_of(block, plane, upper, upper_block, lower):
-        extra = BLOCKS + jnp.maximum(plane, 0) * units
-        late = lower[pl.ds(extra, units)].reshape(UPPER, TILE)
-        top = jnp.where(plane >= 0, late, upper[upper_block])
-        return jnp.concatenate([top, lower[block]])
-
-    def body(own_table, partner_table, ladder_ref, upper, lower, mirror_upper, mirror_lower, out_ref):
+def whole_tile(block, plane, upper, upper_block, lower):
+    units = UPPER // (TILE - UPPER)
+    late = lower[pl.ds(BLOCKS + jnp.maximum(plane, 0) * units, units)].reshape(UPPER, TILE)
+    top = jnp.where(plane >= 0, late, upper[upper_block])
+    return jnp.concatenate([top, lower[block]])
+
+
+def by_bands(body, table, full, upper, upper_spec, lower, kind):
+    side = SIDE * TILE
+    band = pl.BlockSpec((TILE, side), lambda i: (i, 0))
+    return pl.pallas_call(
+        body,
+        grid=(SIDE,),
+        out_shape=kind((side, side), F32),
+        in_specs=[SMEM, band, upper_spec, pl.BlockSpec(lower.shape, lambda i: (0, 0, 0))],
+        out_specs=band,
+        compiler_params=pltpu.CompilerParams(vmem_limit_bytes=12 << 20),
+    )(table, full, upper, lower)
+
+
+def plus_own(planes, ladder, upper, lower):
+    def body(table, ladder_ref, upper_ref, lower_ref, out_ref):
         i = pl.program_id(0)
 
         @pl.loop(0, SIDE)
         def _(j):
             cols = pl.ds(pl.multiple_of(j * TILE, TILE), TILE)
-            here, there = i * SIDE + j, j * SIDE + i
-            mine = tile_of(here, own_table[here], upper, j, lower)
-            theirs = tile_of(there, partner_table[there], mirror_upper, there, mirror_lower)
-            out_ref[:, cols] = ladder_ref[:, cols] + mine.astype(F32) - theirs.T.astype(F32)
-
-    side = SIDE * TILE
-    whole = [pl.BlockSpec(a.shape, lambda i: (0, 0, 0)) for a in (own[1], *partner)]
-    return pl.pallas_call(
-        body,
-        grid=(SIDE,),
-        out_shape=jax.ShapeDtypeStruct((side, side), F32),
-        in_specs=[
-            SMEM,
-            SMEM,
-            pl.BlockSpec((TILE, side), lambda i: (i, 0)),
-            pl.BlockSpec((SIDE, UPPER, TILE), lambda i: (i, 0, 0)),
-            *whole,
-        ],
-        out_specs=pl.BlockSpec((TILE, side), lambda i: (i, 0)),
-        compiler_params=pltpu.CompilerParams(vmem_limit_bytes=LIMIT << 20),
-    )(own_planes, partner_planes, ladder, *own, *partner)
+            block = i * SIDE + j
+            tile = whole_tile(block, table[block], upper_ref, j, lower_ref)
+            out_ref[:, cols] = ladder_ref[:, cols] + tile.astype(F32)
+
+    upper_spec = pl.BlockSpec((SIDE, UPPER, TILE), lambda i: (i, 0, 0))
+    return by_bands(body, planes, ladder, upper, upper_spec, lower, jax.ShapeDtypeStruct)
+
+
+def minus_mirror(planes, base, upper, lower):
+    def body(table, base_ref, upper_ref, lower_ref, out_ref):
+        i = pl.program_id(0)
+
+        @pl.loop(0, SIDE)
+        def _(j):
+            cols = pl.ds(pl.multiple_of(j * TILE, TILE), TILE)
+            block = j * SIDE + i
+            tile = whole_tile(block, table[block], upper_ref, block, lower_ref)
+            out_ref[:, cols] = base_ref[:, cols] - tile.T.astype(F32)
+
+    upper_spec = pl.BlockSpec(upper.shape, lambda i: (0, 0, 0))
+    return by_bands(body, planes, base, upper, upper_spec, lower, pltpu.HBM)
 
 
 def pair_product(left_a, right_a, left_b, right_b):
@@ -434,9 +493,10 @@
     lower_own = gathered_lower(slots, jnp.maximum(own_planes, 0), lower)
     lower_partner = lax.ppermute(lower_own, "grp", mirror)
 
+    base = plus_own(own_planes, ladder, upper_own, lower_own)
+
     def fast():
-        own, partner = (upper_own, lower_own), (upper_partner, lower_partner)
-        return assembled(own_planes, partner_planes, ladder, own, partner)
+        return minus_mirror(partner_planes, base, upper_partner, lower_partner)
 
     def slow():
         arrived = exchanged(direct_tiles(direct_blocks, gen_mat, ham_mat))
@@ -447,7 +507,7 @@
         own = gathered(2 * my_dest + my_later.astype(jnp.int32), back)
         partner = in_bands(lax.ppermute(own, "grp", mirror))
         nowhere = jnp.full((BLOCKS,), -1, jnp.int32)
-        return assembled(nowhere, nowhere, ladder, in_bands(own), partner)
+        return minus_mirror(nowhere, plus_own(nowhere, ladder, *in_bands(own)), *partner)
 
     return lax.cond(crowded, slow, fast)[None, None]
 

time: 298 us -> 291 us (0.977)
  waiting for transfers between devices: 157 us -> 152 us
  local copies, waits for them, and re-layouts: 8.35 us -> 5.16 us
    ppermute x1, waiting for transfers between devices: 23.4 us -> 17 us  [on_device(): lower_partner = lax.ppermute(lower_own, 'grp', mirror)]
    unnamed x31 -> x27, local copies, waits for them, and re-layouts: 6.31 us -> 3.13 us
    pallas_call x7 -> x8, Pallas kernels: 29.1 us -> 30 us  [the longest x6 18.7 us: kernel_call(): pl.pallas_call(body, out_shape=outs, in_specs=[SMEM] * len(tables) + [HBM...]
  transfers between devices with their start and end apart: 26 -> 26, of which waited for: 10 -> 10; matrix products, arithmetic and copies ran while one was open for 5% -> 5% of each run, Pallas kernels for 3% -> 4%
where the time goes in v1:
time: 291 us; the launch traced here: 290 us
  waiting for transfers between devices  152 us (52%)
  starting transfers between devices  82.1 us (28%)
  Pallas kernels  30 us (10%)
  matrix products  12.8 us (4%)
  other arithmetic  7.11 us (2%)
  local copies, waits for them, and re-layouts  5.16 us (2%)
    ppermute x7, waiting for transfers between devices, z_shift(): return lax.ppermute(value, 'chan', pairs)  85.8 us
    ppermute x14, starting transfers between devices, x_shift(): return lax.ppermute(value, 'chan', pairs)  35.6 us
    ppermute x14, waiting for transfers between devices, x_shift(): return lax.ppermute(value, 'chan', pairs)  34.2 us
    all_to_all x3, starting transfers between devices, exchanged(): lax.all_to_all(value, 'chan', split_axis=0, concat_axis=0, tiled=True)  30.6 us
    pallas_call x6, Pallas kernels, kernel_call(): pl.pallas_call(body, out_shape=outs, in_specs=[SMEM] * len(tables) + [HBM...  18.7 us
    ppermute x1, waiting for transfers between devices, on_device(): lower_partner = lax.ppermute(lower_own, 'grp', mirror)  17 us
    all_to_all x3, waiting for transfers between devices, exchanged(): lax.all_to_all(value, 'chan', split_axis=0, concat_axis=0, tiled=True)  14.6 us
    ppermute x7, starting transfers between devices, z_shift(): return lax.ppermute(value, 'chan', pairs)  13.1 us
  transfers between devices with their start and end apart: 26, of which 10 were waited for; matrix products, arithmetic and copies ran while one was open for 5% of the time, Pallas kernels for 4%

profile of v1, /device:TPU:1, one launch (start us, length us, event | category | flops | bytes accessed | tf_op | source)
XLA Modules:
  0.0 289.9 jit_solution(18054588552691363483)
XLA Ops:
  1.6 1.6 select_reduce_fusion.1
  4.5 5.0 %shard_map.57 = (bf16[64,2,128,128]{3,2,1,0:T(8,128)(2,1)}, bf16[2,128,128]{2,1,0:T(8,128)(2,1)S(1)}, bf16[2,128,128]{2,1,0:T(8,128)(2,1)S(1)}, bf16[2,128,128]{...) custom-call(s32[64]{0:T(128)S(1)} %select_reduce_fusion.4.main_table, ...), custom_call_target="tpu_custom_call" | custom-call | tf_op jit(solution)/shard_map/pallas_call | solution.py:59
  9.5 13.3 %all-to-all-start.2 = ((bf16[64,2,128,128]{3,2,1,0:T(8,128)(2,1)}), bf16[64,2,128,128]{3,2,1,0:T(8,128)(2,1)}, u32[]{:S(2)}, u32[]{:S(2)}) async-start(bf16[64,2,128,128]{3,2,1,0:T(8,128)(2,1)} %get-tuple-element.98), calls=%async_computation.2 | async-start | bytes 8388608 | tf_op jit(solution)/shard_map/all_to_all | solution.py:52
  22.9 1.4 collective-permute-start.1
  24.3 2.1 collective-permute-start.2
  26.4 2.4 collective-permute-start.3
  28.8 2.1 collective-permute-start.4
  30.8 2.4 collective-permute-start.5
  33.8 1.1 dynamic-slice_reduce_fusion.1
  34.9 2.3 convert_reduce_fusion
  39.5 76.1 %collective-permute-done.1 = bf16[2,128,128]{2,1,0:T(8,128)(2,1)S(1)} collective-permute-done((bf16[2,128,128]{2,1,0:T(8,128)(2,1)S(1)}, bf16[2,128,128]{2,1,0:T(8,128)(2,1)S(1)}, u32[]{:S(2)}, u32[]{:S(2)}) %collective-permute-start.1) | collective-permute-done | bytes 65568 | tf_op jit(solution)/shard_map/ppermute | solution.py:38
  115.6 2.0 collective-permute-start.6
  117.6 2.4 collective-permute-done.2
  120.7 2.1 collective-permute-done.3
  122.9 5.1 %collective-permute-done.4 = bf16[2,128,128]{2,1,0:T(8,128)(2,1)S(1)} collective-permute-done((bf16[2,128,128]{2,1,0:T(8,128)(2,1)S(1)}, bf16[2,128,128]{2,1,0:T(8,128)(2,1)S(1)}, u32[]{:S(2)}, u32[]{:S(2)}) %collective-permute-start.4) | collective-permute-done | bytes 65568 | tf_op jit(solution)/shard_map/ppermute | solution.py:38
  128.1 1.3 collective-permute-start.8
  129.4 2.6 collective-permute-start.9
  132.0 1.1 collective-permute-start.10
  133.3 4.0 %fusion.1 = f32[896,896]{1,0:T(8,128)S(1)} fusion(bf16[1,1,896,896]{3,2,1,0:T(8,128)(2,1)} %param.7, f32[896]{0:T(1024)S(1)} %reduce.4, bf16[1,1,896,896]{3,2,1,0:T(8,128)(2,1)} %param.8), kind=kOutput, calls=%fused_computation.10 | convolution fusion | flops 1441054720 | bytes 6426112 | tf_op jit(solution)/shard_map/dot_general | solution.py:366
  137.4 3.4 %collective-permute-start.11 = (bf16[8,2,128,128]{3,2,1,0:T(8,128)(2,1)S(1)}, bf16[8,2,128,128]{3,2,1,0:T(8,128)(2,1)S(1)}, u32[]{:S(2)}, u32[]{:S(2)}) collective-permute-start(bf16[8,2,128,128]{3,2,1,0:T(8,128)(2,1)S(1)} %bitcast_dynamic-update-slice_fusion.refs_0_), channel_id=1, source_target_pairs={{0,1},{1,0},{2,3},{3,2},{4,5},{5,4},{6,7},{7,6},{8,9},{9,8},{10,11... | collective-permute-start | bytes 1572872 | tf_op jit(solution)/shard_map/ppermute | solution.py:48
  140.8 4.7 %collective-permute-start.12 = (bf16[8,2,128,128]{3,2,1,0:T(8,128)(2,1)S(1)}, bf16[8,2,128,128]{3,2,1,0:T(8,128)(2,1)S(1)}, u32[]{:S(2)}, u32[]{:S(2)}) collective-permute-start(bf16[8,2,128,128]{3,2,1,0:T(8,128)(2,1)S(1)} %collective-permute-done.8.refs_1_), channel_id=1, source_target_pairs={{0,1},{1,0},{2,3},{3,2},{4,5},{5,4},{6,7},{7,6},{8,9},{9,8},{10,11... | collective-permute-start | bytes 1572872 | tf_op jit(solution)/shard_map/ppermute | solution.py:48
  145.5 7.2 %collective-permute-done.9.refs_2_ = bf16[8,2,128,128]{3,2,1,0:T(8,128)(2,1)S(1)} collective-permute-done((bf16[8,2,128,128]{3,2,1,0:T(8,128)(2,1)S(1)}, bf16[8,2,128,128]{3,2,1,0:T(8,128)(2,1)S(1)}, u32[]{:S(2)}, u32[]{:S(2)}) %collective-permute-start.9) | collective-permute-done | bytes 524320 | tf_op jit(solution)/shard_map/ppermute | solution.py:48
  152.8 3.4 %collective-permute-start.13 = (bf16[8,2,128,128]{3,2,1,0:T(8,128)(2,1)S(1)}, bf16[8,2,128,128]{3,2,1,0:T(8,128)(2,1)}, u32[]{:S(2)}, u32[]{:S(2)}) collective-permute-start(bf16[8,2,128,128]{3,2,1,0:T(8,128)(2,1)S(1)} %collective-permute-done.9.refs_2_), channel_id=1, source_target_pairs={{0,1},{1,0},{2,3},{3,2},{4,5},{5,4},{6,7},{7,6},{8,9},{9,8},{10,11... | collective-permute-start | bytes 1572872 | tf_op jit(solution)/shard_map/ppermute | solution.py:48
  156.2 3.7 %convolution_subtract_fusion.1.ladder_ref = f32[896,896]{1,0:T(8,128)} fusion(f32[896,896]{1,0:T(8,128)S(1)} %fusion.1, bf16[1,1,896,896]{3,2,1,0:T(8,128)(2,1)S(1)} %copy-done.9, f32[896]{0:T(1024)S(1)} %reduce.4, bf16[1,1,896,896]{3,2,1,0:T(8,128)(2,1)S(1)} %copy-done.8), kind=kOutput, calls=%fused_computation.8 | convolution fusion | flops 1441857536 | bytes 9637376 | tf_op jit(solution)/shard_map/dot_general | solution.py:367
  159.9 5.0 %shard_map.58 = (bf16[896,896]{1,0:T(8,128)(2,1)S(1)}, bf16[896,896]{1,0:T(8,128)(2,1)S(1)}) custom-call(s32[64]{0:T(128)S(1)} %get-tuple-element.153.main_table, s32[64]{0:T(128)S(1)} %select_reduce_fusion.2.second_table, bf16[64,2,128,128]{3,2,1,0:T(8,128)(2,1)} %all-to-all-done.2.main_ref, ...), custom_call_target="tpu_custom_call" | custom-call | tf_op jit(solution)/shard_map/pallas_call | solution.py:59
  164.9 2.0 fusion.41
  166.9 2.0 convolution_subtract_fusion.cross_ref
  169.0 3.1 %shard_map.59 = (bf16[64,112,128]{2,1,0:T(8,128)(2,1)}, bf16[64,16,128]{2,1,0:T(8,128)(2,1)S(1)}, bf16[64,16,128]{2,1,0:T(8,128)(2,1)S(1)}, bf16[64,16,128]{2,1,...) custom-call(s32[64]{0:T(128)S(1)} %broadcast_maximum_fusion.2.main_t, ...), custom_call_target="tpu_custom_call" | custom-call | tf_op jit(solution)/shard_map/pallas_call | solution.py:59
  174.2 7.5 %all-to-all-start.3 = ((bf16[64,112,128]{2,1,0:T(8,128)(2,1)}), bf16[64,112,128]{2,1,0:T(8,128)(2,1)S(1)}, u32[]{:S(2)}, u32[]{:S(2)}) async-start(bf16[64,112,128]{2,1,0:T(8,128)(2,1)} %get-tuple-element.117), calls=%async_computation.3 | async-start | bytes 3670016 | tf_op jit(solution)/shard_map/all_to_all | solution.py:52
  181.7 1.4 collective-permute-start.15
  183.2 2.6 collective-permute-start.16
  185.8 1.1 collective-permute-start.17
  186.9 1.2 collective-permute-start.18
  188.4 8.3 %collective-permute-done.15.refs_1_ = bf16[64,16,128]{2,1,0:T(8,128)(2,1)S(1)} collective-permute-done((bf16[64,16,128]{2,1,0:T(8,128)(2,1)}, bf16[64,16,128]{2,1,0:T(8,128)(2,1)S(1)}, u32[]{:S(2)}, u32[]{:S(2)}) %collective-permute-start.15) | collective-permute-done | bytes 262176 | tf_op jit(solution)/shard_map/ppermute | solution.py:48
  196.7 12.4 %collective-permute-start.20 = (bf16[64,16,128]{2,1,0:T(8,128)(2,1)S(1)}, bf16[64,16,128]{2,1,0:T(8,128)(2,1)S(1)}, u32[]{:S(2)}, u32[]{:S(2)}) collective-permute-start(bf16[64,16,128]{2,1,0:T(8,128)(2,1)S(1)} %get-tuple-element.125), channel_id=1, source_target_pairs={{0,33},{1,32},{2,35},{3,34},{4,37},{5,36},{6,39},{7,38},{8,41},{9,... | collective-permute-start | bytes 786440 | tf_op jit(solution)/shard_map/ppermute | solution.py:48
  209.1 10.1 %collective-permute-done.19.refs_5_ = bf16[64,16,128]{2,1,0:T(8,128)(2,1)S(1)} collective-permute-done((bf16[64,16,128]{2,1,0:T(8,128)(2,1)S(1)}, bf16[64,16,128]{2,1,0:T(8,128)(2,1)S(1)}, u32[]{:S(2)}, u32[]{:S(2)}) %collective-permute-start.19) | collective-permute-done | bytes 262176 | tf_op jit(solution)/shard_map/ppermute | solution.py:48
  219.3 8.5 %collective-permute-done.20.refs_6_ = bf16[64,16,128]{2,1,0:T(8,128)(2,1)S(1)} collective-permute-done((bf16[64,16,128]{2,1,0:T(8,128)(2,1)S(1)}, bf16[64,16,128]{2,1,0:T(8,128)(2,1)S(1)}, u32[]{:S(2)}, u32[]{:S(2)}) %collective-permute-start.20) | collective-permute-done | bytes 262176 | tf_op jit(solution)/shard_map/ppermute | solution.py:48
  227.8 2.3 shard_map.61
  230.2 9.8 %all-to-all-start.4 = ((bf16[64,32,128]{2,1,0:T(8,128)(2,1)}), bf16[64,32,128]{2,1,0:T(8,128)(2,1)}, u32[]{:S(2)}, u32[]{:S(2)}) async-start(bf16[64,32,128]{2,1,0:T(8,128)(2,1)} %shard_map.61), calls=%async_computation.4 | async-start | bytes 1048576 | tf_op jit(solution)/shard_map/all_to_all | solution.py:52
  240.0 1.2 shard_map.60.upper_ref
  241.2 1.4 collective-permute-start.22
  242.6 14.6 %all-to-all-done.4.main_ref = bf16[64,32,128]{2,1,0:T(8,128)(2,1)} async-done(((bf16[64,32,128]{2,1,0:T(8,128)(2,1)}), bf16[64,32,128]{2,1,0:T(8,128)(2,1)}, u32[]{:S(2)}, u32[]{:S(2)}) %all-to-all-start.4) | async-done | bytes 524320 | tf_op jit(solution)/shard_map/all_to_all | solution.py:52
  257.2 2.0 shard_map.62.lower_ref
  259.2 1.4 collective-permute-start.23
  260.6 4.7 %shard_map.63 = f32[896,896]{1,0:T(8,128)S(1)} custom-call(s32[49]{0:T(128)S(1)} %get-tuple-element.103.table, f32[896,896]{1,0:T(8,128)} %convolution_subtract_fusion.1.ladder_ref, bf16[49,112,128]{2,1,0:T(8,128)(2,1)S(1)} %shard_map.60.upper_ref, bf16[105,16,128]{2,1,0:T(8,128)(2,1)S(1)} %shard_map.62.lower_ref), custom_call_target="tpu_custom_call" | custom-call | tf_op jit(solution)/shard_map/pallas_call | solution.py:325
  265.3 17.0 %collective-permute-done.23 = bf16[105,16,128]{2,1,0:T(8,128)(2,1)S(1)} collective-permute-done((bf16[105,16,128]{2,1,0:T(8,128)(2,1)S(1)}, bf16[105,16,128]{2,1,0:T(8,128)(2,1)S(1)}, u32[]{:S(2)}, u32[]{:S(2)}) %collective-permute-start.23) | collective-permute-done | bytes 430112 | tf_op jit(solution)/shard_map/ppermute | solution.py:494
  282.3 6.6 %conditional.1 = (f32[1,1,896,896]{3,2,1,0:T(8,128)}) conditional(s32[]{:T(128)} %convert_element_type.63, (s32[49]{0:T(128)S(1)}, f32[896,896]{1,0:T(8,128)S(1)}, bf16[49,112,128]{2,1,0:T(8,128)(2,1)}, bf16[105,16,128]{2,1,0:T(8,128)(2,1)S(1)}) %tuple.17, (s32[49]{0:T(128)S(1)}, pred[49]{0:T(512)(128)(4,1)S(1)}, s32[64]{0:T(128)S(1)}, ...), branch_computations={%region_17.18_spmd, %region_18.20_spmd} | conditional | flops 9555 | bytes 78049072 | solution.py:512
  282.3 6.6 %branch_0_fun.1 = f32[896,896]{1,0:T(8,128)} custom-call(s32[49]{0:T(128)S(1)} %get-tuple-element.47.table, f32[896,896]{1,0:T(8,128)S(1)} %get-tuple-element.48.base_ref, bf16[49,112,128]{2,1,0:T(8,128)(2,1)} %get-tuple-element.49.upper_ref, bf16[105,16,128]{2,1,0:T(8,128)(2,1)S(1)} %get-tuple-element.50.lower_ref), custom_call_target="tpu_custom_call" | custom-call | tf_op jit(solution)/shard_map/cond/branch_0_fun/pallas_call | solution.py:325
  (88 shorter events, 9.4 us)
Async XLA Ops:
  0.0 34.8 %copy-start = (s32[4,64,49]{1,0,2:T(4,128)S(1)}, s32[4,64,49]{1,0,2:T(4,128)}, u32[]{:S(2)}) copy-start(s32[4,64,49]{1,0,2:T(4,128)} %param.11) | copy-start | bytes 150532
  9.5 23.7 %copy-start.10 = (s32[4,64,49,1]{1,3,2,0:T(1,128)S(1)}, s32[4,64,49,1]{1,3,2,0:T(1,128)}, u32[]{:S(2)}) copy-start(s32[4,64,49,1]{1,3,2,0:T(1,128)} %param.10) | copy-start | bytes 150532
  9.5 29.9 %copy-start.11 = (f32[1,1,896]{2,1,0:T(1,128)S(1)}, f32[1,1,896]{2,1,0:T(1,128)}, u32[]{:S(2)}) copy-start(f32[1,1,896]{2,1,0:T(1,128)} %param.9) | copy-start | bytes 10756
  9.5 150.3 %all-to-all-start.2 = ((bf16[64,2,128,128]{3,2,1,0:T(8,128)(2,1)}), bf16[64,2,128,128]{3,2,1,0:T(8,128)(2,1)}, u32[]{:S(2)}, u32[]{:S(2)}) async-start(bf16[64,2,128,128]{3,2,1,0:T(8,128)(2,1)} %get-tuple-element.98), calls=%async_computation.2 | async-start | bytes 8388608 | tf_op jit(solution)/shard_map/all_to_all | solution.py:52
  22.9 92.7 %collective-permute-start.1 = (bf16[2,128,128]{2,1,0:T(8,128)(2,1)S(1)}, bf16[2,128,128]{2,1,0:T(8,128)(2,1)S(1)}, u32[]{:S(2)}, u32[]{:S(2)}) collective-permute-start(bf16[2,128,128]{2,1,0:T(8,128)(2,1)S(1)} %get-tuple-element.108), channel_id=1, source_target_pairs={{0,2},{1,3},{2,4},{3,5},{4,6},{5,7},{6,8},{7,9},{8,10},{9,11},{10,... | collective-permute-start | bytes 196616 | tf_op jit(solution)/shard_map/ppermute | solution.py:38
  24.3 95.7 %collective-permute-start.2 = (bf16[2,128,128]{2,1,0:T(8,128)(2,1)S(1)}, bf16[2,128,128]{2,1,0:T(8,128)(2,1)S(1)}, u32[]{:S(2)}, u32[]{:S(2)}) collective-permute-start(bf16[2,128,128]{2,1,0:T(8,128)(2,1)S(1)} %get-tuple-element.109), channel_id=1, source_target_pairs={{0,4},{1,5},{2,6},{3,7},{4,8},{5,9},{6,10},{7,11},{8,12},{9,13},{1... | collective-permute-start | bytes 196616 | tf_op jit(solution)/shard_map/ppermute | solution.py:38
  26.4 96.5 %collective-permute-start.3 = (bf16[2,128,128]{2,1,0:T(8,128)(2,1)S(1)}, bf16[2,128,128]{2,1,0:T(8,128)(2,1)S(1)}, u32[]{:S(2)}, u32[]{:S(2)}) collective-permute-start(bf16[2,128,128]{2,1,0:T(8,128)(2,1)S(1)} %get-tuple-element.110), channel_id=1, source_target_pairs={{0,6},{1,7},{2,8},{3,9},{4,10},{5,11},{6,12},{7,13},{8,14},{9,15},... | collective-permute-start | bytes 196616 | tf_op jit(solution)/shard_map/ppermute | solution.py:38
  28.8 99.2 %collective-permute-start.4 = (bf16[2,128,128]{2,1,0:T(8,128)(2,1)S(1)}, bf16[2,128,128]{2,1,0:T(8,128)(2,1)S(1)}, u32[]{:S(2)}, u32[]{:S(2)}) collective-permute-start(bf16[2,128,128]{2,1,0:T(8,128)(2,1)S(1)} %get-tuple-element.111), channel_id=1, source_target_pairs={{0,8},{1,9},{2,10},{3,11},{4,12},{5,13},{6,14},{7,15},{8,0},{9,1},... | collective-permute-start | bytes 196616 | tf_op jit(solution)/shard_map/ppermute | solution.py:38
  30.8 97.2 %collective-permute-start.5 = (bf16[2,128,128]{2,1,0:T(8,128)(2,1)S(1)}, bf16[2,128,128]{2,1,0:T(8,128)(2,1)S(1)}, u32[]{:S(2)}, u32[]{:S(2)}) collective-permute-start(bf16[2,128,128]{2,1,0:T(8,128)(2,1)S(1)} %get-tuple-element.112), channel_id=1, source_target_pairs={{0,10},{1,11},{2,12},{3,13},{4,14},{5,15},{6,0},{7,1},{8,2},{9,3},... | collective-permute-start | bytes 196616 | tf_op jit(solution)/shard_map/ppermute | solution.py:38
  115.6 12.5 %collective-permute-start.6 = (bf16[2,128,128]{2,1,0:T(8,128)(2,1)S(1)}, bf16[2,128,128]{2,1,0:T(8,128)(2,1)S(1)}, u32[]{:S(2)}, u32[]{:S(2)}) collective-permute-start(bf16[2,128,128]{2,1,0:T(8,128)(2,1)S(1)} %get-tuple-element.113), channel_id=1, source_target_pairs={{0,12},{1,13},{2,14},{3,15},{4,0},{5,1},{6,2},{7,3},{8,4},{9,5},{1... | collective-permute-start | bytes 196616 | tf_op jit(solution)/shard_map/ppermute | solution.py:38
  120.0 8.1 %collective-permute-start.7 = (bf16[2,128,128]{2,1,0:T(8,128)(2,1)S(1)}, bf16[2,128,128]{2,1,0:T(8,128)(2,1)S(1)}, u32[]{:S(2)}, u32[]{:S(2)}) collective-permute-start(bf16[2,128,128]{2,1,0:T(8,128)(2,1)S(1)} %get-tuple-element.114), channel_id=1, source_target_pairs={{0,14},{1,15},{2,0},{3,1},{4,2},{5,3},{6,4},{7,5},{8,6},{9,7},{10,... | collective-permute-start | bytes 196616 | tf_op jit(solution)/shard_map/ppermute | solution.py:38
  128.1 12.7 %collective-permute-start.8 = (bf16[8,2,128,128]{3,2,1,0:T(8,128)(2,1)S(1)}, bf16[8,2,128,128]{3,2,1,0:T(8,128)(2,1)S(1)}, u32[]{:S(2)}, u32[]{:S(2)}) collective-permute-start(bf16[8,2,128,128]{3,2,1,0:T(8,128)(2,1)S(1)} %bitcast_dynamic-update-slice_fusion.refs_0_), channel_id=1, source_target_pairs={{0,16},{1,17},{2,18},{3,19},{4,20},{5,21},{6,22},{7,23},{8,24},{9,... | collective-permute-start | bytes 1572872 | tf_op jit(solution)/shard_map/ppermute | solution.py:48
  129.4 23.3 %collective-permute-start.9 = (bf16[8,2,128,128]{3,2,1,0:T(8,128)(2,1)S(1)}, bf16[8,2,128,128]{3,2,1,0:T(8,128)(2,1)S(1)}, u32[]{:S(2)}, u32[]{:S(2)}) collective-permute-start(bf16[8,2,128,128]{3,2,1,0:T(8,128)(2,1)S(1)} %bitcast_dynamic-update-slice_fusion.refs_0_), channel_id=1, source_target_pairs={{0,32},{1,33},{2,34},{3,35},{4,36},{5,37},{6,38},{7,39},{8,40},{9,... | collective-permute-start | bytes 1572872 | tf_op jit(solution)/shard_map/ppermute | solution.py:48
  132.0 24.1 %collective-permute-start.10 = (bf16[8,2,128,128]{3,2,1,0:T(8,128)(2,1)S(1)}, bf16[8,2,128,128]{3,2,1,0:T(8,128)(2,1)S(1)}, u32[]{:S(2)}, u32[]{:S(2)}) collective-permute-start(bf16[8,2,128,128]{3,2,1,0:T(8,128)(2,1)S(1)} %bitcast_dynamic-update-slice_fusion.refs_0_), channel_id=1, source_target_pairs={{0,48},{1,49},{2,50},{3,51},{4,52},{5,53},{6,54},{7,55},{8,56},{9,... | collective-permute-start | bytes 1572872 | tf_op jit(solution)/shard_map/ppermute | solution.py:48
  133.3 22.9 %copy-start.8 = (bf16[1,1,896,896]{3,2,1,0:T(8,128)(2,1)S(1)}, bf16[1,1,896,896]{3,2,1,0:T(8,128)(2,1)}, u32[]{:S(2)}) copy-start(bf16[1,1,896,896]{3,2,1,0:T(8,128)(2,1)} %param.7) | copy-start | bytes 4816900
  133.3 22.9 %copy-start.9 = (bf16[1,1,896,896]{3,2,1,0:T(8,128)(2,1)S(1)}, bf16[1,1,896,896]{3,2,1,0:T(8,128)(2,1)}, u32[]{:S(2)}) copy-start(bf16[1,1,896,896]{3,2,1,0:T(8,128)(2,1)} %param.8) | copy-start | bytes 4816900
  137.4 22.5 %collective-permute-start.11 = (bf16[8,2,128,128]{3,2,1,0:T(8,128)(2,1)S(1)}, bf16[8,2,128,128]{3,2,1,0:T(8,128)(2,1)S(1)}, u32[]{:S(2)}, u32[]{:S(2)}) collective-permute-start(bf16[8,2,128,128]{3,2,1,0:T(8,128)(2,1)S(1)} %bitcast_dynamic-update-slice_fusion.refs_0_), channel_id=1, source_target_pairs={{0,1},{1,0},{2,3},{3,2},{4,5},{5,4},{6,7},{7,6},{8,9},{9,8},{10,11... | collective-permute-start | bytes 1572872 | tf_op jit(solution)/shard_map/ppermute | solution.py:48
  140.8 19.1 %collective-permute-start.12 = (bf16[8,2,128,128]{3,2,1,0:T(8,128)(2,1)S(1)}, bf16[8,2,128,128]{3,2,1,0:T(8,128)(2,1)S(1)}, u32[]{:S(2)}, u32[]{:S(2)}) collective-permute-start(bf16[8,2,128,128]{3,2,1,0:T(8,128)(2,1)S(1)} %collective-permute-done.8.refs_1_), channel_id=1, source_target_pairs={{0,1},{1,0},{2,3},{3,2},{4,5},{5,4},{6,7},{7,6},{8,9},{9,8},{10,11... | collective-permute-start | bytes 1572872 | tf_op jit(solution)/shard_map/ppermute | solution.py:48
  152.8 7.1 %collective-permute-start.13 = (bf16[8,2,128,128]{3,2,1,0:T(8,128)(2,1)S(1)}, bf16[8,2,128,128]{3,2,1,0:T(8,128)(2,1)}, u32[]{:S(2)}, u32[]{:S(2)}) collective-permute-start(bf16[8,2,128,128]{3,2,1,0:T(8,128)(2,1)S(1)} %collective-permute-done.9.refs_2_), channel_id=1, source_target_pairs={{0,1},{1,0},{2,3},{3,2},{4,5},{5,4},{6,7},{7,6},{8,9},{9,8},{10,11... | collective-permute-start | bytes 1572872 | tf_op jit(solution)/shard_map/ppermute | solution.py:48
  156.1 3.8 %collective-permute-start.14 = (bf16[8,2,128,128]{3,2,1,0:T(8,128)(2,1)S(1)}, bf16[8,2,128,128]{3,2,1,0:T(8,128)(2,1)}, u32[]{:S(2)}, u32[]{:S(2)}) collective-permute-start(bf16[8,2,128,128]{3,2,1,0:T(8,128)(2,1)S(1)} %collective-permute-done.10.refs_3_), channel_id=1, source_target_pairs={{0,1},{1,0},{2,3},{3,2},{4,5},{5,4},{6,7},{7,6},{8,9},{9,8},{10,11... | collective-permute-start | bytes 1572872 | tf_op jit(solution)/shard_map/ppermute | solution.py:48
  172.1 0.7 copy-start.4
  172.8 0.7 copy-start.5
  173.5 0.7 copy-start.6
  174.2 55.9 %all-to-all-start.3 = ((bf16[64,112,128]{2,1,0:T(8,128)(2,1)}), bf16[64,112,128]{2,1,0:T(8,128)(2,1)S(1)}, u32[]{:S(2)}, u32[]{:S(2)}) async-start(bf16[64,112,128]{2,1,0:T(8,128)(2,1)} %get-tuple-element.117), calls=%async_computation.3 | async-start | bytes 3670016 | tf_op jit(solution)/shard_map/all_to_all | solution.py:52
  181.7 14.9 %collective-permute-start.15 = (bf16[64,16,128]{2,1,0:T(8,128)(2,1)}, bf16[64,16,128]{2,1,0:T(8,128)(2,1)S(1)}, u32[]{:S(2)}, u32[]{:S(2)}) collective-permute-start(bf16[64,16,128]{2,1,0:T(8,128)(2,1)} %copy-done.6), channel_id=1, source_target_pairs={{0,16},{1,17},{2,18},{3,19},{4,20},{5,21},{6,22},{7,23},{8,24},{9,... | collective-permute-start | bytes 786440 | tf_op jit(solution)/shard_map/ppermute | solution.py:48
  183.2 25.9 %collective-permute-start.16 = (bf16[64,16,128]{2,1,0:T(8,128)(2,1)}, bf16[64,16,128]{2,1,0:T(8,128)(2,1)S(1)}, u32[]{:S(2)}, u32[]{:S(2)}) collective-permute-start(bf16[64,16,128]{2,1,0:T(8,128)(2,1)} %copy-done.5), channel_id=1, source_target_pairs={{0,32},{1,33},{2,34},{3,35},{4,36},{5,37},{6,38},{7,39},{8,40},{9,... | collective-permute-start | bytes 786440 | tf_op jit(solution)/shard_map/ppermute | solution.py:48
  185.8 23.3 %collective-permute-start.17 = (bf16[64,16,128]{2,1,0:T(8,128)(2,1)}, bf16[64,16,128]{2,1,0:T(8,128)(2,1)S(1)}, u32[]{:S(2)}, u32[]{:S(2)}) collective-permute-start(bf16[64,16,128]{2,1,0:T(8,128)(2,1)} %copy-done.4), channel_id=1, source_target_pairs={{0,48},{1,49},{2,50},{3,51},{4,52},{5,53},{6,54},{7,55},{8,56},{9,... | collective-permute-start | bytes 786440 | tf_op jit(solution)/shard_map/ppermute | solution.py:48
  186.9 22.3 %collective-permute-start.18 = (bf16[64,16,128]{2,1,0:T(8,128)(2,1)S(1)}, bf16[64,16,128]{2,1,0:T(8,128)(2,1)S(1)}, u32[]{:S(2)}, u32[]{:S(2)}) collective-permute-start(bf16[64,16,128]{2,1,0:T(8,128)(2,1)S(1)} %get-tuple-element.123), channel_id=1, source_target_pairs={{0,1},{1,0},{2,3},{3,2},{4,5},{5,4},{6,7},{7,6},{8,9},{9,8},{10,11... | collective-permute-start | bytes 786440 | tf_op jit(solution)/shard_map/ppermute | solution.py:48
  188.1 31.2 %collective-permute-start.19 = (bf16[64,16,128]{2,1,0:T(8,128)(2,1)S(1)}, bf16[64,16,128]{2,1,0:T(8,128)(2,1)S(1)}, u32[]{:S(2)}, u32[]{:S(2)}) collective-permute-start(bf16[64,16,128]{2,1,0:T(8,128)(2,1)S(1)} %get-tuple-element.124), channel_id=1, source_target_pairs={{0,17},{1,16},{2,19},{3,18},{4,21},{5,20},{6,23},{7,22},{8,25},{9,... | collective-permute-start | bytes 786440 | tf_op jit(solution)/shard_map/ppermute | solution.py:48
  196.7 31.2 %collective-permute-start.20 = (bf16[64,16,128]{2,1,0:T(8,128)(2,1)S(1)}, bf16[64,16,128]{2,1,0:T(8,128)(2,1)S(1)}, u32[]{:S(2)}, u32[]{:S(2)}) collective-permute-start(bf16[64,16,128]{2,1,0:T(8,128)(2,1)S(1)} %get-tuple-element.125), channel_id=1, source_target_pairs={{0,33},{1,32},{2,35},{3,34},{4,37},{5,36},{6,39},{7,38},{8,41},{9,... | collective-permute-start | bytes 786440 | tf_op jit(solution)/shard_map/ppermute | solution.py:48
  209.1 18.7 %collective-permute-start.21 = (bf16[64,16,128]{2,1,0:T(8,128)(2,1)S(1)}, bf16[64,16,128]{2,1,0:T(8,128)(2,1)S(1)}, u32[]{:S(2)}, u32[]{:S(2)}) collective-permute-start(bf16[64,16,128]{2,1,0:T(8,128)(2,1)S(1)} %get-tuple-element.126), channel_id=1, source_target_pairs={{0,49},{1,48},{2,51},{3,50},{4,53},{5,52},{6,55},{7,54},{8,57},{9,... | collective-permute-start | bytes 786440 | tf_op jit(solution)/shard_map/ppermute | solution.py:48
  230.2 27.0 %all-to-all-start.4 = ((bf16[64,32,128]{2,1,0:T(8,128)(2,1)}), bf16[64,32,128]{2,1,0:T(8,128)(2,1)}, u32[]{:S(2)}, u32[]{:S(2)}) async-start(bf16[64,32,128]{2,1,0:T(8,128)(2,1)} %shard_map.61), calls=%async_computation.4 | async-start | bytes 1048576 | tf_op jit(solution)/shard_map/all_to_all | solution.py:52
  241.2 41.1 %collective-permute-start.22 = (bf16[49,112,128]{2,1,0:T(8,128)(2,1)S(1)}, bf16[49,112,128]{2,1,0:T(8,128)(2,1)}, u32[]{:S(2)}, u32[]{:S(2)}) collective-permute-start(bf16[49,112,128]{2,1,0:T(8,128)(2,1)S(1)} %shard_map.60.upper_ref), channel_id=1, source_target_pairs={{0,64},{64,0},{128,192},{192,128},{1,65},{65,1},{129,193},{193,129... | collective-permute-start | bytes 4214792 | tf_op jit(solution)/shard_map/ppermute | solution.py:492
  259.2 23.2 %collective-permute-start.23 = (bf16[105,16,128]{2,1,0:T(8,128)(2,1)S(1)}, bf16[105,16,128]{2,1,0:T(8,128)(2,1)S(1)}, u32[]{:S(2)}, u32[]{:S(2)}) collective-permute-start(bf16[105,16,128]{2,1,0:T(8,128)(2,1)S(1)} %shard_map.62.lower_ref), channel_id=1, source_target_pairs={{0,64},{64,0},{128,192},{192,128},{1,65},{65,1},{129,193},{193,129... | collective-permute-start | bytes 1290248 | tf_op jit(solution)/shard_map/ppermute | solution.py:494
  289.0 0.9 copy-start.1

commit v2 on v1

--- a/solution.py
+++ b/solution.py
@@ -14,6 +14,7 @@
 UPPER = 112
 LIMIT = 24
 PIECE = TILE // (X * CORE)
+HOPS = (0, 4, 3, 5, 2, 6, 1, 7)
 RELATIVE = [(step, flip) for flip in range(CORE) for step in range(X)]
 F32, BF16 = jnp.float32, jnp.bfloat16
 
@@ -190,18 +191,15 @@
             copies.append(pltpu.make_async_copy(held.at[where], upper_ref.at[where], done.at[part]))
             copies[-1].start()
 
-        @pl.loop(0, CHAN)
+        @pl.loop(0, CHAN, unroll=4)
         def _(slot):
             block = second_table[slot]
-
-            @pl.when(block >= 0)
-            def _():
-                row = (block // SIDE) * TILE
-                col = pl.multiple_of((block % SIDE) * TILE, TILE)
-                for part in range(count):
-                    first = pl.multiple_of(row + piece_table[part] * PIECE, PIECE)
-                    rows = cross_ref[pl.ds(first, PIECE), pl.ds(col, TILE)]
-                    piece_refs[part][slot] = rows.astype(BF16)
+            row = (block // SIDE) * TILE
+            col = pl.multiple_of((block % SIDE) * TILE, TILE)
+            for part in range(count):
+                first = pl.multiple_of(row + piece_table[part] * PIECE, PIECE)
+                rows = cross_ref[pl.ds(first, PIECE), pl.ds(col, TILE)]
+                piece_refs[part][slot] = rows.astype(BF16)
 
         for copy in copies:
             copy.wait()
@@ -416,28 +414,33 @@
         row, col = rank // Z, rank % Z
         return chan_of(row // CORE, col, row % CORE)
 
-    rank, _ = homes_of(owners)
-    dest = jnp.sum(jnp.where(owners[:, :, None] == names, home_of(rank), 0), axis=-1)
-    alike = (owners[:, None, :] == owners[:, :, None]) & (blocks[None, :] < blocks[:, None])
-    later = jnp.any(alike, axis=-1)
-
-    my_dest = lax.dynamic_index_in_dim(dest, me, 0, keepdims=False)
-    my_later = lax.dynamic_index_in_dim(later, me, 0, keepdims=False)
+    home = home_of(homes_of(owners)[0])
+
+    def routes(named):
+        dest = jnp.sum(jnp.where(named[..., None] == names, home, 0), axis=-1)
+        alike = named[..., None, :] == named[..., :, None]
+        return dest, jnp.any(alike & (blocks[None, :] < blocks[:, None]), axis=-1)
+
+    my_dest, my_later = routes(lax.dynamic_index_in_dim(owners, me, 0, keepdims=False))
     my_plane = (my_dest // CORE) % Z
     to_home = my_dest[None, :] == names[:, None]
     main_blocks = jnp.max(jnp.where(to_home & ~my_later, blocks, 0), axis=1)
     direct_blocks = jnp.max(jnp.where(to_home & my_later, blocks, 0), axis=1)
-    to_plane = my_plane[None, :] == ((my_z + steps) % Z)[:, None]
+    hops = jnp.array(HOPS, jnp.int32)
+    to_plane = my_plane[None, :] == ((my_z + hops) % Z)[:, None]
     second_blocks = jnp.max(jnp.where(to_plane & my_later, blocks, 0), axis=1)
 
     main_send, *second_send = send_tiles(main_blocks, second_blocks, gen_mat, ham_mat)
-    second_send[0], owner_late = lax.optimization_barrier((second_send[0], owner_all))
+    second_send[0], owner_late, owners_late = lax.optimization_barrier(
+        (second_send[0], owner_all, owners)
+    )
+    dest, later = routes(owners_late)
     rank_all, double_all = homes_of(owner_late)
     planes_all = ((rank_all % Z)[..., None] == steps).astype(BF16)
     in_plane = jnp.einsum("gck,gkt->gct", double_all.astype(BF16), planes_all, preferred_element_type=F32)
     crowded = jnp.max(in_plane) > 1.5
 
-    shifted = [z_shift(second_send[s], s) for s in range(1, Z)]
+    shifted = [z_shift(second_send[i], HOPS[i]) for i in range(1, Z)]
     main = exchanged(main_send)
     ladder = ladder_term(gen_mat, ham_mat, occ_row)
 
@@ -450,7 +453,7 @@
     second_place = jnp.max(jnp.where(here & later, offsets, -1), axis=1)
     flips = jnp.arange(CORE, dtype=jnp.int32)[:, None]
     shifts = jnp.arange(X, dtype=jnp.int32)[None, :]
-    from_z = (my_z - steps) % Z
+    from_z = (my_z - hops) % Z
     came_from = chan_of(((my_x - shifts) % X)[..., None], from_z, (my_core ^ flips)[..., None]).reshape(-1)
     place_in = jnp.sum(jnp.where(came_from[:, None] == names, second_place, 0), axis=1)
 
@@ -476,7 +479,9 @@
     back_main_offsets = jnp.maximum(main_place, 0)
 
     piece_of = (((my_x + shifts) % X) * CORE + (my_core ^ flips)).reshape(-1)
-    upper_send, lower_rows, *pieces = back_tiles(back_main_offsets, second_place, piece_of, cross)
+    upper_send, lower_rows, *pieces = back_tiles(
+        back_main_offsets, jnp.maximum(second_place, 0), piece_of, cross
+    )
     upper = exchanged(upper_send)
     routed = [
         x_shift(piece, step, flip) if step or flip else piece

time: 291 us -> 291 us (level)
  waiting for transfers between devices: 152 us -> 139 us
  starting transfers between devices: 82.1 us -> 91.2 us
    ppermute x7, waiting for transfers between devices: 85.8 us -> 76.6 us  [z_shift(): return lax.ppermute(value, 'chan', pairs)]
    ppermute x7, starting transfers between devices: 13.1 us -> 19.2 us  [z_shift(): return lax.ppermute(value, 'chan', pairs)]
    ppermute x14, waiting for transfers between devices: 34.2 us -> 31.2 us  [x_shift(): return lax.ppermute(value, 'chan', pairs)]
  transfers between devices with their start and end apart: 26 -> 26, of which waited for: 10 -> 9; matrix products, arithmetic and copies ran while one was open for 5% -> 5% of each run, Pallas kernels for 4% -> 4%
where the time goes in v2:
time: 291 us; the launch traced here: 290 us
  waiting for transfers between devices  139 us (48%)
  starting transfers between devices  91.2 us (31%)
  Pallas kernels  30.6 us (11%)
  matrix products  12.7 us (4%)
  other arithmetic  7.75 us (3%)
  local copies, waits for them, and re-layouts  6.98 us (2%)
    ppermute x7, waiting for transfers between devices, z_shift(): return lax.ppermute(value, 'chan', pairs)  76.6 us
    ppermute x14, starting transfers between devices, x_shift(): return lax.ppermute(value, 'chan', pairs)  38.5 us
    ppermute x14, waiting for transfers between devices, x_shift(): return lax.ppermute(value, 'chan', pairs)  31.2 us
    all_to_all x3, starting transfers between devices, exchanged(): lax.all_to_all(value, 'chan', split_axis=0, concat_axis=0, tiled=True)  30.6 us
    pallas_call x6, Pallas kernels, kernel_call(): pl.pallas_call(body, out_shape=outs, in_specs=[SMEM] * len(tables) + [HBM...  19.3 us
    ppermute x7, starting transfers between devices, z_shift(): return lax.ppermute(value, 'chan', pairs)  19.2 us
    ppermute x1, waiting for transfers between devices, on_device(): lower_partner = lax.ppermute(lower_own, 'grp', mirror)  16.9 us
    all_to_all x3, waiting for transfers between devices, exchanged(): lax.all_to_all(value, 'chan', split_axis=0, concat_axis=0, tiled=True)  14.5 us
  transfers between devices with their start and end apart: 26, of which 9 were waited for; matrix products, arithmetic and copies ran while one was open for 5% of the time, Pallas kernels for 4%

profile of v2, /device:TPU:1, one launch (start us, length us, event | category | flops | bytes accessed | tf_op | source)
XLA Modules:
  0.0 289.7 jit_solution(14983382471951426506)
XLA Ops:
  0.0 0.8 constant_dynamic-slice_fusion.1
  1.6 1.8 dynamic-slice_reduce_fusion.1
  4.8 5.0 %shard_map.66 = (bf16[64,2,128,128]{3,2,1,0:T(8,128)(2,1)}, bf16[2,128,128]{2,1,0:T(8,128)(2,1)S(1)}, bf16[2,128,128]{2,1,0:T(8,128)(2,1)S(1)}, bf16[2,128,128]{...) custom-call(s32[64]{0:T(128)S(1)} %select_reduce_fusion.4.main_table, ...), custom_call_target="tpu_custom_call" | custom-call | tf_op jit(solution)/shard_map/pallas_call | solution.py:60
  9.8 13.3 %all-to-all-start.2 = ((bf16[64,2,128,128]{3,2,1,0:T(8,128)(2,1)}), bf16[64,2,128,128]{3,2,1,0:T(8,128)(2,1)}, u32[]{:S(2)}, u32[]{:S(2)}) async-start(bf16[64,2,128,128]{3,2,1,0:T(8,128)(2,1)} %get-tuple-element.99), calls=%async_computation.2 | async-start | bytes 8388608 | tf_op jit(solution)/shard_map/all_to_all | solution.py:53
  23.1 5.3 %collective-permute-start.1 = (bf16[2,128,128]{2,1,0:T(8,128)(2,1)S(1)}, bf16[2,128,128]{2,1,0:T(8,128)(2,1)S(1)}, u32[]{:S(2)}, u32[]{:S(2)}) collective-permute-start(bf16[2,128,128]{2,1,0:T(8,128)(2,1)S(1)} %get-tuple-element.110), channel_id=1, source_target_pairs={{0,8},{1,9},{2,10},{3,11},{4,12},{5,13},{6,14},{7,15},{8,0},{9,1},... | collective-permute-start | bytes 196616 | tf_op jit(solution)/shard_map/ppermute | solution.py:39
  28.8 4.2 %collective-permute-start.3 = (bf16[2,128,128]{2,1,0:T(8,128)(2,1)S(1)}, bf16[2,128,128]{2,1,0:T(8,128)(2,1)S(1)}, u32[]{:S(2)}, u32[]{:S(2)}) collective-permute-start(bf16[2,128,128]{2,1,0:T(8,128)(2,1)S(1)} %get-tuple-element.112), channel_id=1, source_target_pairs={{0,10},{1,11},{2,12},{3,13},{4,14},{5,15},{6,0},{7,1},{8,2},{9,3},... | collective-permute-start | bytes 196616 | tf_op jit(solution)/shard_map/ppermute | solution.py:39
  33.2 3.3 %collective-permute-start.5 = (bf16[2,128,128]{2,1,0:T(8,128)(2,1)S(1)}, bf16[2,128,128]{2,1,0:T(8,128)(2,1)S(1)}, u32[]{:S(2)}, u32[]{:S(2)}) collective-permute-start(bf16[2,128,128]{2,1,0:T(8,128)(2,1)S(1)} %get-tuple-element.114), channel_id=1, source_target_pairs={{0,12},{1,13},{2,14},{3,15},{4,0},{5,1},{6,2},{7,3},{8,4},{9,5},{1... | collective-permute-start | bytes 196616 | tf_op jit(solution)/shard_map/ppermute | solution.py:39
  37.0 1.1 dynamic-slice_reduce_fusion
  38.2 2.3 convert_reduce_fusion
  41.8 1.6 select_reduce_fusion.1
  45.0 75.4 %collective-permute-done.1 = bf16[2,128,128]{2,1,0:T(8,128)(2,1)S(1)} collective-permute-done((bf16[2,128,128]{2,1,0:T(8,128)(2,1)S(1)}, bf16[2,128,128]{2,1,0:T(8,128)(2,1)S(1)}, u32[]{:S(2)}, u32[]{:S(2)}) %collective-permute-start.1) | collective-permute-done | bytes 65568 | tf_op jit(solution)/shard_map/ppermute | solution.py:39
  120.3 1.7 collective-permute-start.6
  122.1 4.0 %collective-permute-start.7 = (bf16[2,128,128]{2,1,0:T(8,128)(2,1)S(1)}, bf16[2,128,128]{2,1,0:T(8,128)(2,1)S(1)}, u32[]{:S(2)}, u32[]{:S(2)}) collective-permute-start(bf16[2,128,128]{2,1,0:T(8,128)(2,1)S(1)} %get-tuple-element.116), channel_id=1, source_target_pairs={{0,14},{1,15},{2,0},{3,1},{4,2},{5,3},{6,4},{7,5},{8,6},{9,7},{10,... | collective-permute-start | bytes 196616 | tf_op jit(solution)/shard_map/ppermute | solution.py:39
  126.6 0.9 collective-permute-done.7
  127.5 1.2 collective-permute-start.8
  128.7 2.6 collective-permute-start.9
  131.3 1.1 collective-permute-start.10
  132.6 4.0 %fusion.1 = f32[896,896]{1,0:T(8,128)S(1)} fusion(bf16[1,1,896,896]{3,2,1,0:T(8,128)(2,1)} %param.8, f32[896]{0:T(1024)S(1)} %reduce.1, bf16[1,1,896,896]{3,2,1,0:T(8,128)(2,1)} %param.9), kind=kOutput, calls=%fused_computation.10 | convolution fusion | flops 1441054720 | bytes 6426112 | tf_op jit(solution)/shard_map/dot_general | solution.py:364
  136.6 4.8 %collective-permute-start.11 = (bf16[8,2,128,128]{3,2,1,0:T(8,128)(2,1)S(1)}, bf16[8,2,128,128]{3,2,1,0:T(8,128)(2,1)S(1)}, u32[]{:S(2)}, u32[]{:S(2)}) collective-permute-start(bf16[8,2,128,128]{3,2,1,0:T(8,128)(2,1)S(1)} %bitcast_dynamic-update-slice_fusion.refs_0_), channel_id=1, source_target_pairs={{0,1},{1,0},{2,3},{3,2},{4,5},{5,4},{6,7},{7,6},{8,9},{9,8},{10,11... | collective-permute-start | bytes 1572872 | tf_op jit(solution)/shard_map/ppermute | solution.py:49
  141.4 4.9 %collective-permute-start.12 = (bf16[8,2,128,128]{3,2,1,0:T(8,128)(2,1)S(1)}, bf16[8,2,128,128]{3,2,1,0:T(8,128)(2,1)S(1)}, u32[]{:S(2)}, u32[]{:S(2)}) collective-permute-start(bf16[8,2,128,128]{3,2,1,0:T(8,128)(2,1)S(1)} %collective-permute-done.8.refs_1_), channel_id=1, source_target_pairs={{0,1},{1,0},{2,3},{3,2},{4,5},{5,4},{6,7},{7,6},{8,9},{9,8},{10,11... | collective-permute-start | bytes 1572872 | tf_op jit(solution)/shard_map/ppermute | solution.py:49
  146.4 4.3 %collective-permute-done.9.refs_2_ = bf16[8,2,128,128]{3,2,1,0:T(8,128)(2,1)S(1)} collective-permute-done((bf16[8,2,128,128]{3,2,1,0:T(8,128)(2,1)S(1)}, bf16[8,2,128,128]{3,2,1,0:T(8,128)(2,1)S(1)}, u32[]{:S(2)}, u32[]{:S(2)}) %collective-permute-start.9) | collective-permute-done | bytes 524320 | tf_op jit(solution)/shard_map/ppermute | solution.py:49
  150.6 4.8 %collective-permute-start.13 = (bf16[8,2,128,128]{3,2,1,0:T(8,128)(2,1)S(1)}, bf16[8,2,128,128]{3,2,1,0:T(8,128)(2,1)}, u32[]{:S(2)}, u32[]{:S(2)}) collective-permute-start(bf16[8,2,128,128]{3,2,1,0:T(8,128)(2,1)S(1)} %collective-permute-done.9.refs_2_), channel_id=1, source_target_pairs={{0,1},{1,0},{2,3},{3,2},{4,5},{5,4},{6,7},{7,6},{8,9},{9,8},{10,11... | collective-permute-start | bytes 1572872 | tf_op jit(solution)/shard_map/ppermute | solution.py:49
  155.4 3.7 %convolution_subtract_fusion.1.ladder_ref = f32[896,896]{1,0:T(8,128)} fusion(f32[896,896]{1,0:T(8,128)S(1)} %fusion.1, bf16[1,1,896,896]{3,2,1,0:T(8,128)(2,1)S(1)} %copy-done.9, f32[896]{0:T(1024)S(1)} %reduce.1, bf16[1,1,896,896]{3,2,1,0:T(8,128)(2,1)S(1)} %copy-done.8), kind=kOutput, calls=%fused_computation.8 | convolution fusion | flops 1441857536 | bytes 9637376 | tf_op jit(solution)/shard_map/dot_general | solution.py:365
  159.2 5.0 %shard_map.67 = (bf16[896,896]{1,0:T(8,128)(2,1)S(1)}, bf16[896,896]{1,0:T(8,128)(2,1)S(1)}) custom-call(s32[64]{0:T(128)S(1)} %get-tuple-element.155.main_table, s32[64]{0:T(128)S(1)} %select_reduce_fusion.2.second_table, bf16[64,2,128,128]{3,2,1,0:T(8,128)(2,1)} %all-to-all-done.2.main_ref, ...), custom_call_target="tpu_custom_call" | custom-call | tf_op jit(solution)/shard_map/pallas_call | solution.py:60
  164.2 2.0 fusion.36
  166.2 2.0 convolution_subtract_fusion.cross_ref
  168.2 3.7 %shard_map.68 = (bf16[64,112,128]{2,1,0:T(8,128)(2,1)}, bf16[64,16,128]{2,1,0:T(8,128)(2,1)S(1)}, bf16[64,16,128]{2,1,0:T(8,128)(2,1)S(1)}, bf16[64,16,128]{2,1,...) custom-call(s32[64]{0:T(128)S(1)} %broadcast_maximum_fusion.3.main_t, ...), custom_call_target="tpu_custom_call" | custom-call | tf_op jit(solution)/shard_map/pallas_call | solution.py:60
  174.0 7.5 %all-to-all-start.3 = ((bf16[64,112,128]{2,1,0:T(8,128)(2,1)}), bf16[64,112,128]{2,1,0:T(8,128)(2,1)S(1)}, u32[]{:S(2)}, u32[]{:S(2)}) async-start(bf16[64,112,128]{2,1,0:T(8,128)(2,1)} %get-tuple-element.119), calls=%async_computation.3 | async-start | bytes 3670016 | tf_op jit(solution)/shard_map/all_to_all | solution.py:53
  181.6 1.4 collective-permute-start.15
  183.0 2.6 collective-permute-start.16
  185.6 1.1 collective-permute-start.17
  186.7 1.2 collective-permute-start.18
  188.2 8.3 %collective-permute-done.15.refs_1_ = bf16[64,16,128]{2,1,0:T(8,128)(2,1)S(1)} collective-permute-done((bf16[64,16,128]{2,1,0:T(8,128)(2,1)}, bf16[64,16,128]{2,1,0:T(8,128)(2,1)S(1)}, u32[]{:S(2)}, u32[]{:S(2)}) %collective-permute-start.15) | collective-permute-done | bytes 262176 | tf_op jit(solution)/shard_map/ppermute | solution.py:49
  196.5 12.4 %collective-permute-start.20 = (bf16[64,16,128]{2,1,0:T(8,128)(2,1)S(1)}, bf16[64,16,128]{2,1,0:T(8,128)(2,1)S(1)}, u32[]{:S(2)}, u32[]{:S(2)}) collective-permute-start(bf16[64,16,128]{2,1,0:T(8,128)(2,1)S(1)} %get-tuple-element.127), channel_id=1, source_target_pairs={{0,33},{1,32},{2,35},{3,34},{4,37},{5,36},{6,39},{7,38},{8,41},{9,... | collective-permute-start | bytes 786440 | tf_op jit(solution)/shard_map/ppermute | solution.py:49
  209.0 10.1 %collective-permute-done.19.refs_5_ = bf16[64,16,128]{2,1,0:T(8,128)(2,1)S(1)} collective-permute-done((bf16[64,16,128]{2,1,0:T(8,128)(2,1)S(1)}, bf16[64,16,128]{2,1,0:T(8,128)(2,1)S(1)}, u32[]{:S(2)}, u32[]{:S(2)}) %collective-permute-start.19) | collective-permute-done | bytes 262176 | tf_op jit(solution)/shard_map/ppermute | solution.py:49
  219.1 8.5 %collective-permute-done.20.refs_6_ = bf16[64,16,128]{2,1,0:T(8,128)(2,1)S(1)} collective-permute-done((bf16[64,16,128]{2,1,0:T(8,128)(2,1)S(1)}, bf16[64,16,128]{2,1,0:T(8,128)(2,1)S(1)}, u32[]{:S(2)}, u32[]{:S(2)}) %collective-permute-start.20) | collective-permute-done | bytes 262176 | tf_op jit(solution)/shard_map/ppermute | solution.py:49
  227.6 2.3 shard_map.70
  230.0 9.8 %all-to-all-start.4 = ((bf16[64,32,128]{2,1,0:T(8,128)(2,1)}), bf16[64,32,128]{2,1,0:T(8,128)(2,1)}, u32[]{:S(2)}, u32[]{:S(2)}) async-start(bf16[64,32,128]{2,1,0:T(8,128)(2,1)} %shard_map.70), calls=%async_computation.4 | async-start | bytes 1048576 | tf_op jit(solution)/shard_map/all_to_all | solution.py:53
  239.8 1.2 shard_map.69.upper_ref
  241.0 1.5 collective-permute-start.22
  242.5 14.5 %all-to-all-done.4.main_ref = bf16[64,32,128]{2,1,0:T(8,128)(2,1)} async-done(((bf16[64,32,128]{2,1,0:T(8,128)(2,1)}), bf16[64,32,128]{2,1,0:T(8,128)(2,1)}, u32[]{:S(2)}, u32[]{:S(2)}) %all-to-all-start.4) | async-done | bytes 524320 | tf_op jit(solution)/shard_map/all_to_all | solution.py:53
  257.0 2.0 shard_map.71.lower_ref
  259.0 1.5 collective-permute-start.23
  260.5 4.7 %shard_map.72 = f32[896,896]{1,0:T(8,128)S(1)} custom-call(s32[49]{0:T(128)S(1)} %get-tuple-element.104.table, f32[896,896]{1,0:T(8,128)} %convolution_subtract_fusion.1.ladder_ref, bf16[49,112,128]{2,1,0:T(8,128)(2,1)S(1)} %shard_map.69.upper_ref, bf16[105,16,128]{2,1,0:T(8,128)(2,1)S(1)} %shard_map.71.lower_ref), custom_call_target="tpu_custom_call" | custom-call | tf_op jit(solution)/shard_map/pallas_call | solution.py:323
  265.2 16.9 %collective-permute-done.23 = bf16[105,16,128]{2,1,0:T(8,128)(2,1)S(1)} collective-permute-done((bf16[105,16,128]{2,1,0:T(8,128)(2,1)S(1)}, bf16[105,16,128]{2,1,0:T(8,128)(2,1)S(1)}, u32[]{:S(2)}, u32[]{:S(2)}) %collective-permute-start.23) | collective-permute-done | bytes 430112 | tf_op jit(solution)/shard_map/ppermute | solution.py:499
  282.2 6.6 %conditional.1 = (f32[1,1,896,896]{3,2,1,0:T(8,128)}) conditional(s32[]{:T(128)} %convert_element_type.63, (s32[49]{0:T(128)S(1)}, f32[896,896]{1,0:T(8,128)S(1)}, bf16[49,112,128]{2,1,0:T(8,128)(2,1)}, bf16[105,16,128]{2,1,0:T(8,128)(2,1)S(1)}) %tuple.17, (s32[49]{0:T(128)S(1)}, pred[49]{0:T(512)(128)(4,1)S(1)}, s32[64]{0:T(128)S(1)}, ...), branch_computations={%region_19.20_spmd, %region_20.22_spmd} | conditional | flops 9555 | bytes 78049072 | solution.py:517
  282.2 6.6 %branch_0_fun.1 = f32[896,896]{1,0:T(8,128)} custom-call(s32[49]{0:T(128)S(1)} %get-tuple-element.47.table, f32[896,896]{1,0:T(8,128)S(1)} %get-tuple-element.48.base_ref, bf16[49,112,128]{2,1,0:T(8,128)(2,1)} %get-tuple-element.49.upper_ref, bf16[105,16,128]{2,1,0:T(8,128)(2,1)S(1)} %get-tuple-element.50.lower_ref), custom_call_target="tpu_custom_call" | custom-call | tf_op jit(solution)/shard_map/cond/branch_0_fun/pallas_call | solution.py:323
  288.8 0.9 copy-done.1
  (91 shorter events, 8.6 us)
Async XLA Ops:
  0.0 38.1 %copy-start = (s32[4,64,49]{1,0,2:T(4,128)S(1)}, s32[4,64,49]{1,0,2:T(4,128)}, u32[]{:S(2)}) copy-start(s32[4,64,49]{1,0,2:T(4,128)} %param.12) | copy-start | bytes 150532
  9.8 26.7 %copy-start.10 = (s32[4,64,49,1]{1,3,2,0:T(1,128)S(1)}, s32[4,64,49,1]{1,3,2,0:T(1,128)}, u32[]{:S(2)}) copy-start(s32[4,64,49,1]{1,3,2,0:T(1,128)} %param.11) | copy-start | bytes 150532
  9.8 35.1 %copy-start.11 = (f32[1,1,896]{2,1,0:T(1,128)S(1)}, f32[1,1,896]{2,1,0:T(1,128)}, u32[]{:S(2)}) copy-start(f32[1,1,896]{2,1,0:T(1,128)} %param.10) | copy-start | bytes 10756
  9.8 149.3 %all-to-all-start.2 = ((bf16[64,2,128,128]{3,2,1,0:T(8,128)(2,1)}), bf16[64,2,128,128]{3,2,1,0:T(8,128)(2,1)}, u32[]{:S(2)}, u32[]{:S(2)}) async-start(bf16[64,2,128,128]{3,2,1,0:T(8,128)(2,1)} %get-tuple-element.99), calls=%async_computation.2 | async-start | bytes 8388608 | tf_op jit(solution)/shard_map/all_to_all | solution.py:53
  23.1 97.2 %collective-permute-start.1 = (bf16[2,128,128]{2,1,0:T(8,128)(2,1)S(1)}, bf16[2,128,128]{2,1,0:T(8,128)(2,1)S(1)}, u32[]{:S(2)}, u32[]{:S(2)}) collective-permute-start(bf16[2,128,128]{2,1,0:T(8,128)(2,1)S(1)} %get-tuple-element.110), channel_id=1, source_target_pairs={{0,8},{1,9},{2,10},{3,11},{4,12},{5,13},{6,14},{7,15},{8,0},{9,1},... | collective-permute-start | bytes 196616 | tf_op jit(solution)/shard_map/ppermute | solution.py:39
  28.5 93.6 %collective-permute-start.2 = (bf16[2,128,128]{2,1,0:T(8,128)(2,1)S(1)}, bf16[2,128,128]{2,1,0:T(8,128)(2,1)S(1)}, u32[]{:S(2)}, u32[]{:S(2)}) collective-permute-start(bf16[2,128,128]{2,1,0:T(8,128)(2,1)S(1)} %get-tuple-element.111), channel_id=1, source_target_pairs={{0,6},{1,7},{2,8},{3,9},{4,10},{5,11},{6,12},{7,13},{8,14},{9,15},... | collective-permute-start | bytes 196616 | tf_op jit(solution)/shard_map/ppermute | solution.py:39
  28.8 97.4 %collective-permute-start.3 = (bf16[2,128,128]{2,1,0:T(8,128)(2,1)S(1)}, bf16[2,128,128]{2,1,0:T(8,128)(2,1)S(1)}, u32[]{:S(2)}, u32[]{:S(2)}) collective-permute-start(bf16[2,128,128]{2,1,0:T(8,128)(2,1)S(1)} %get-tuple-element.112), channel_id=1, source_target_pairs={{0,10},{1,11},{2,12},{3,13},{4,14},{5,15},{6,0},{7,1},{8,2},{9,3},... | collective-permute-start | bytes 196616 | tf_op jit(solution)/shard_map/ppermute | solution.py:39
  33.0 93.2 %collective-permute-start.4 = (bf16[2,128,128]{2,1,0:T(8,128)(2,1)S(1)}, bf16[2,128,128]{2,1,0:T(8,128)(2,1)S(1)}, u32[]{:S(2)}, u32[]{:S(2)}) collective-permute-start(bf16[2,128,128]{2,1,0:T(8,128)(2,1)S(1)} %get-tuple-element.113), channel_id=1, source_target_pairs={{0,4},{1,5},{2,6},{3,7},{4,8},{5,9},{6,10},{7,11},{8,12},{9,13},{1... | collective-permute-start | bytes 196616 | tf_op jit(solution)/shard_map/ppermute | solution.py:39
  33.2 93.0 %collective-permute-start.5 = (bf16[2,128,128]{2,1,0:T(8,128)(2,1)S(1)}, bf16[2,128,128]{2,1,0:T(8,128)(2,1)S(1)}, u32[]{:S(2)}, u32[]{:S(2)}) collective-permute-start(bf16[2,128,128]{2,1,0:T(8,128)(2,1)S(1)} %get-tuple-element.114), channel_id=1, source_target_pairs={{0,12},{1,13},{2,14},{3,15},{4,0},{5,1},{6,2},{7,3},{8,4},{9,5},{1... | collective-permute-start | bytes 196616 | tf_op jit(solution)/shard_map/ppermute | solution.py:39
  120.3 6.2 %collective-permute-start.6 = (bf16[2,128,128]{2,1,0:T(8,128)(2,1)S(1)}, bf16[2,128,128]{2,1,0:T(8,128)(2,1)S(1)}, u32[]{:S(2)}, u32[]{:S(2)}) collective-permute-start(bf16[2,128,128]{2,1,0:T(8,128)(2,1)S(1)} %get-tuple-element.115), channel_id=1, source_target_pairs={{0,2},{1,3},{2,4},{3,5},{4,6},{5,7},{6,8},{7,9},{8,10},{9,11},{10,... | collective-permute-start | bytes 196616 | tf_op jit(solution)/shard_map/ppermute | solution.py:39
  122.1 5.4 %collective-permute-start.7 = (bf16[2,128,128]{2,1,0:T(8,128)(2,1)S(1)}, bf16[2,128,128]{2,1,0:T(8,128)(2,1)S(1)}, u32[]{:S(2)}, u32[]{:S(2)}) collective-permute-start(bf16[2,128,128]{2,1,0:T(8,128)(2,1)S(1)} %get-tuple-element.116), channel_id=1, source_target_pairs={{0,14},{1,15},{2,0},{3,1},{4,2},{5,3},{6,4},{7,5},{8,6},{9,7},{10,... | collective-permute-start | bytes 196616 | tf_op jit(solution)/shard_map/ppermute | solution.py:39
  127.5 14.0 %collective-permute-start.8 = (bf16[8,2,128,128]{3,2,1,0:T(8,128)(2,1)S(1)}, bf16[8,2,128,128]{3,2,1,0:T(8,128)(2,1)S(1)}, u32[]{:S(2)}, u32[]{:S(2)}) collective-permute-start(bf16[8,2,128,128]{3,2,1,0:T(8,128)(2,1)S(1)} %bitcast_dynamic-update-slice_fusion.refs_0_), channel_id=1, source_target_pairs={{0,16},{1,17},{2,18},{3,19},{4,20},{5,21},{6,22},{7,23},{8,24},{9,... | collective-permute-start | bytes 1572872 | tf_op jit(solution)/shard_map/ppermute | solution.py:49
  128.7 22.0 %collective-permute-start.9 = (bf16[8,2,128,128]{3,2,1,0:T(8,128)(2,1)S(1)}, bf16[8,2,128,128]{3,2,1,0:T(8,128)(2,1)S(1)}, u32[]{:S(2)}, u32[]{:S(2)}) collective-permute-start(bf16[8,2,128,128]{3,2,1,0:T(8,128)(2,1)S(1)} %bitcast_dynamic-update-slice_fusion.refs_0_), channel_id=1, source_target_pairs={{0,32},{1,33},{2,34},{3,35},{4,36},{5,37},{6,38},{7,39},{8,40},{9,... | collective-permute-start | bytes 1572872 | tf_op jit(solution)/shard_map/ppermute | solution.py:49
  131.3 24.1 %collective-permute-start.10 = (bf16[8,2,128,128]{3,2,1,0:T(8,128)(2,1)S(1)}, bf16[8,2,128,128]{3,2,1,0:T(8,128)(2,1)S(1)}, u32[]{:S(2)}, u32[]{:S(2)}) collective-permute-start(bf16[8,2,128,128]{3,2,1,0:T(8,128)(2,1)S(1)} %bitcast_dynamic-update-slice_fusion.refs_0_), channel_id=1, source_target_pairs={{0,48},{1,49},{2,50},{3,51},{4,52},{5,53},{6,54},{7,55},{8,56},{9,... | collective-permute-start | bytes 1572872 | tf_op jit(solution)/shard_map/ppermute | solution.py:49
  132.5 22.9 %copy-start.8 = (bf16[1,1,896,896]{3,2,1,0:T(8,128)(2,1)S(1)}, bf16[1,1,896,896]{3,2,1,0:T(8,128)(2,1)}, u32[]{:S(2)}) copy-start(bf16[1,1,896,896]{3,2,1,0:T(8,128)(2,1)} %param.8) | copy-start | bytes 4816900
  132.5 22.9 %copy-start.9 = (bf16[1,1,896,896]{3,2,1,0:T(8,128)(2,1)S(1)}, bf16[1,1,896,896]{3,2,1,0:T(8,128)(2,1)}, u32[]{:S(2)}) copy-start(bf16[1,1,896,896]{3,2,1,0:T(8,128)(2,1)} %param.9) | copy-start | bytes 4816900
  136.6 22.5 %collective-permute-start.11 = (bf16[8,2,128,128]{3,2,1,0:T(8,128)(2,1)S(1)}, bf16[8,2,128,128]{3,2,1,0:T(8,128)(2,1)S(1)}, u32[]{:S(2)}, u32[]{:S(2)}) collective-permute-start(bf16[8,2,128,128]{3,2,1,0:T(8,128)(2,1)S(1)} %bitcast_dynamic-update-slice_fusion.refs_0_), channel_id=1, source_target_pairs={{0,1},{1,0},{2,3},{3,2},{4,5},{5,4},{6,7},{7,6},{8,9},{9,8},{10,11... | collective-permute-start | bytes 1572872 | tf_op jit(solution)/shard_map/ppermute | solution.py:49
  141.4 17.7 %collective-permute-start.12 = (bf16[8,2,128,128]{3,2,1,0:T(8,128)(2,1)S(1)}, bf16[8,2,128,128]{3,2,1,0:T(8,128)(2,1)S(1)}, u32[]{:S(2)}, u32[]{:S(2)}) collective-permute-start(bf16[8,2,128,128]{3,2,1,0:T(8,128)(2,1)S(1)} %collective-permute-done.8.refs_1_), channel_id=1, source_target_pairs={{0,1},{1,0},{2,3},{3,2},{4,5},{5,4},{6,7},{7,6},{8,9},{9,8},{10,11... | collective-permute-start | bytes 1572872 | tf_op jit(solution)/shard_map/ppermute | solution.py:49
  150.6 8.5 %collective-permute-start.13 = (bf16[8,2,128,128]{3,2,1,0:T(8,128)(2,1)S(1)}, bf16[8,2,128,128]{3,2,1,0:T(8,128)(2,1)}, u32[]{:S(2)}, u32[]{:S(2)}) collective-permute-start(bf16[8,2,128,128]{3,2,1,0:T(8,128)(2,1)S(1)} %collective-permute-done.9.refs_2_), channel_id=1, source_target_pairs={{0,1},{1,0},{2,3},{3,2},{4,5},{5,4},{6,7},{7,6},{8,9},{9,8},{10,11... | collective-permute-start | bytes 1572872 | tf_op jit(solution)/shard_map/ppermute | solution.py:49
  155.4 3.7 %collective-permute-start.14 = (bf16[8,2,128,128]{3,2,1,0:T(8,128)(2,1)S(1)}, bf16[8,2,128,128]{3,2,1,0:T(8,128)(2,1)}, u32[]{:S(2)}, u32[]{:S(2)}) collective-permute-start(bf16[8,2,128,128]{3,2,1,0:T(8,128)(2,1)S(1)} %collective-permute-done.10.refs_3_), channel_id=1, source_target_pairs={{0,1},{1,0},{2,3},{3,2},{4,5},{5,4},{6,7},{7,6},{8,9},{9,8},{10,11... | collective-permute-start | bytes 1572872 | tf_op jit(solution)/shard_map/ppermute | solution.py:49
  171.9 0.7 copy-start.4
  172.6 0.7 copy-start.5
  173.3 0.7 copy-start.6
  174.0 56.0 %all-to-all-start.3 = ((bf16[64,112,128]{2,1,0:T(8,128)(2,1)}), bf16[64,112,128]{2,1,0:T(8,128)(2,1)S(1)}, u32[]{:S(2)}, u32[]{:S(2)}) async-start(bf16[64,112,128]{2,1,0:T(8,128)(2,1)} %get-tuple-element.119), calls=%async_computation.3 | async-start | bytes 3670016 | tf_op jit(solution)/shard_map/all_to_all | solution.py:53
  181.6 14.9 %collective-permute-start.15 = (bf16[64,16,128]{2,1,0:T(8,128)(2,1)}, bf16[64,16,128]{2,1,0:T(8,128)(2,1)S(1)}, u32[]{:S(2)}, u32[]{:S(2)}) collective-permute-start(bf16[64,16,128]{2,1,0:T(8,128)(2,1)} %copy-done.6), channel_id=1, source_target_pairs={{0,16},{1,17},{2,18},{3,19},{4,20},{5,21},{6,22},{7,23},{8,24},{9,... | collective-permute-start | bytes 786440 | tf_op jit(solution)/shard_map/ppermute | solution.py:49
  183.0 25.9 %collective-permute-start.16 = (bf16[64,16,128]{2,1,0:T(8,128)(2,1)}, bf16[64,16,128]{2,1,0:T(8,128)(2,1)S(1)}, u32[]{:S(2)}, u32[]{:S(2)}) collective-permute-start(bf16[64,16,128]{2,1,0:T(8,128)(2,1)} %copy-done.5), channel_id=1, source_target_pairs={{0,32},{1,33},{2,34},{3,35},{4,36},{5,37},{6,38},{7,39},{8,40},{9,... | collective-permute-start | bytes 786440 | tf_op jit(solution)/shard_map/ppermute | solution.py:49
  185.6 23.3 %collective-permute-start.17 = (bf16[64,16,128]{2,1,0:T(8,128)(2,1)}, bf16[64,16,128]{2,1,0:T(8,128)(2,1)S(1)}, u32[]{:S(2)}, u32[]{:S(2)}) collective-permute-start(bf16[64,16,128]{2,1,0:T(8,128)(2,1)} %copy-done.4), channel_id=1, source_target_pairs={{0,48},{1,49},{2,50},{3,51},{4,52},{5,53},{6,54},{7,55},{8,56},{9,... | collective-permute-start | bytes 786440 | tf_op jit(solution)/shard_map/ppermute | solution.py:49
  186.7 22.3 %collective-permute-start.18 = (bf16[64,16,128]{2,1,0:T(8,128)(2,1)S(1)}, bf16[64,16,128]{2,1,0:T(8,128)(2,1)S(1)}, u32[]{:S(2)}, u32[]{:S(2)}) collective-permute-start(bf16[64,16,128]{2,1,0:T(8,128)(2,1)S(1)} %get-tuple-element.125), channel_id=1, source_target_pairs={{0,1},{1,0},{2,3},{3,2},{4,5},{5,4},{6,7},{7,6},{8,9},{9,8},{10,11... | collective-permute-start | bytes 786440 | tf_op jit(solution)/shard_map/ppermute | solution.py:49
  187.9 31.2 %collective-permute-start.19 = (bf16[64,16,128]{2,1,0:T(8,128)(2,1)S(1)}, bf16[64,16,128]{2,1,0:T(8,128)(2,1)S(1)}, u32[]{:S(2)}, u32[]{:S(2)}) collective-permute-start(bf16[64,16,128]{2,1,0:T(8,128)(2,1)S(1)} %get-tuple-element.126), channel_id=1, source_target_pairs={{0,17},{1,16},{2,19},{3,18},{4,21},{5,20},{6,23},{7,22},{8,25},{9,... | collective-permute-start | bytes 786440 | tf_op jit(solution)/shard_map/ppermute | solution.py:49
  196.5 31.2 %collective-permute-start.20 = (bf16[64,16,128]{2,1,0:T(8,128)(2,1)S(1)}, bf16[64,16,128]{2,1,0:T(8,128)(2,1)S(1)}, u32[]{:S(2)}, u32[]{:S(2)}) collective-permute-start(bf16[64,16,128]{2,1,0:T(8,128)(2,1)S(1)} %get-tuple-element.127), channel_id=1, source_target_pairs={{0,33},{1,32},{2,35},{3,34},{4,37},{5,36},{6,39},{7,38},{8,41},{9,... | collective-permute-start | bytes 786440 | tf_op jit(solution)/shard_map/ppermute | solution.py:49
  208.9 18.7 %collective-permute-start.21 = (bf16[64,16,128]{2,1,0:T(8,128)(2,1)S(1)}, bf16[64,16,128]{2,1,0:T(8,128)(2,1)S(1)}, u32[]{:S(2)}, u32[]{:S(2)}) collective-permute-start(bf16[64,16,128]{2,1,0:T(8,128)(2,1)S(1)} %get-tuple-element.128), channel_id=1, source_target_pairs={{0,49},{1,48},{2,51},{3,50},{4,53},{5,52},{6,55},{7,54},{8,57},{9,... | collective-permute-start | bytes 786440 | tf_op jit(solution)/shard_map/ppermute | solution.py:49
  230.0 27.0 %all-to-all-start.4 = ((bf16[64,32,128]{2,1,0:T(8,128)(2,1)}), bf16[64,32,128]{2,1,0:T(8,128)(2,1)}, u32[]{:S(2)}, u32[]{:S(2)}) async-start(bf16[64,32,128]{2,1,0:T(8,128)(2,1)} %shard_map.70), calls=%async_computation.4 | async-start | bytes 1048576 | tf_op jit(solution)/shard_map/all_to_all | solution.py:53
  241.0 41.1 %collective-permute-start.22 = (bf16[49,112,128]{2,1,0:T(8,128)(2,1)S(1)}, bf16[49,112,128]{2,1,0:T(8,128)(2,1)}, u32[]{:S(2)}, u32[]{:S(2)}) collective-permute-start(bf16[49,112,128]{2,1,0:T(8,128)(2,1)S(1)} %shard_map.69.upper_ref), channel_id=1, source_target_pairs={{0,64},{64,0},{128,192},{192,128},{1,65},{65,1},{129,193},{193,129... | collective-permute-start | bytes 4214792 | tf_op jit(solution)/shard_map/ppermute | solution.py:497
  259.0 23.2 %collective-permute-start.23 = (bf16[105,16,128]{2,1,0:T(8,128)(2,1)S(1)}, bf16[105,16,128]{2,1,0:T(8,128)(2,1)S(1)}, u32[]{:S(2)}, u32[]{:S(2)}) collective-permute-start(bf16[105,16,128]{2,1,0:T(8,128)(2,1)S(1)} %shard_map.71.lower_ref), channel_id=1, source_target_pairs={{0,64},{64,0},{128,192},{192,128},{1,65},{65,1},{129,193},{193,129... | collective-permute-start | bytes 1290248 | tf_op jit(solution)/shard_map/ppermute | solution.py:499
  288.8 0.9 copy-start.1

commit v3 on v2

--- a/solution.py
+++ b/solution.py
@@ -14,7 +14,7 @@
 UPPER = 112
 LIMIT = 24
 PIECE = TILE // (X * CORE)
-HOPS = (0, 4, 3, 5, 2, 6, 1, 7)
+HOPS = tuple(range(Z))
 RELATIVE = [(step, flip) for flip in range(CORE) for step in range(X)]
 F32, BF16 = jnp.float32, jnp.bfloat16
 
@@ -53,7 +53,7 @@
     return lax.all_to_all(value, "chan", split_axis=0, concat_axis=0, tiled=True)
 
 
-def kernel_call(body, tables, arrays, outs, scratch=(), far_in=0, far_out=0):
+def kernel_call(body, tables, arrays, outs, scratch=(), far_in=0, far_out=0, limit=12):
     out_specs = VMEM
     if isinstance(outs, list):
         out_specs = [HBM] * far_out + [VMEM] * (len(outs) - far_out)
@@ -63,7 +63,7 @@
         in_specs=[SMEM] * len(tables) + [HBM] * far_in + [VMEM] * (len(arrays) - far_in),
         out_specs=out_specs,
         scratch_shapes=list(scratch),
-        compiler_params=pltpu.CompilerParams(vmem_limit_bytes=LIMIT << 20),
+        compiler_params=pltpu.CompilerParams(vmem_limit_bytes=limit << 20),
     )(*tables, *arrays)
 
 
@@ -154,12 +154,13 @@
                 def _():
                     total[place] += held[slot].astype(F32)
 
-        @pl.loop(0, BLOCKS)
-        def _(block):
-            rows = pl.ds(pl.multiple_of((block // SIDE) * TILE, TILE), TILE)
-            cols = pl.ds(pl.multiple_of((block % SIDE) * TILE, TILE), TILE)
-            gen_ref[rows, cols] = total[block, 0].astype(BF16)
-            ham_ref[rows, cols] = total[block, 1].astype(BF16)
+        @pl.loop(0, SIDE)
+        def _(i):
+            rows = pl.ds(pl.multiple_of(i * TILE, TILE), TILE)
+            for j in range(SIDE):
+                cols = pl.ds(j * TILE, TILE)
+                gen_ref[rows, cols] = total[i * SIDE + j, 0].astype(BF16)
+                ham_ref[rows, cols] = total[i * SIDE + j, 1].astype(BF16)
 
     outs = [jax.ShapeDtypeStruct((SIDE * TILE, SIDE * TILE), BF16)] * 2
     scratch = [
@@ -168,7 +169,7 @@
         pltpu.SemaphoreType.DMA((CHUNKS,)),
     ]
     tables, arrays = (main_offsets, second_offsets), (main, *seconds)
-    return kernel_call(body, tables, arrays, outs, scratch, far_in=1)
+    return kernel_call(body, tables, arrays, outs, scratch, far_in=1, limit=24)
 
 
 def back_tiles(main_offsets, second_offsets, pieces, cross):
@@ -191,7 +192,7 @@
             copies.append(pltpu.make_async_copy(held.at[where], upper_ref.at[where], done.at[part]))
             copies[-1].start()
 
-        @pl.loop(0, CHAN, unroll=4)
+        @pl.loop(0, CHAN, unroll=2)
         def _(slot):
             block = second_table[slot]
             row = (block // SIDE) * TILE
@@ -209,7 +210,8 @@
         jax.ShapeDtypeStruct((CHAN, TILE - UPPER, TILE), BF16),
     ]
     scratch = [pltpu.VMEM(outs[0].shape, BF16), pltpu.SemaphoreType.DMA((CHUNKS,))]
-    outs += [jax.ShapeDtypeStruct((CHAN, PIECE, TILE), BF16)] * count
+    outs += [jax.ShapeDtypeStruct((CHAN, PIECE, TILE), BF16)]
+    outs += [pltpu.HBM((CHAN, PIECE, TILE), BF16)] * (count - 1)
     tables = (main_offsets, second_offsets, pieces)
     return kernel_call(body, tables, (cross,), outs, scratch, far_out=1)
 
@@ -345,7 +347,7 @@
     return by_bands(body, planes, ladder, upper, upper_spec, lower, jax.ShapeDtypeStruct)
 
 
-def minus_mirror(planes, base, upper, lower):
+def minus_mirror(planes, base, upper, lower, unroll=1):
     def body(table, base_ref, upper_ref, lower_ref, out_ref):
         i = pl.program_id(0)
 
@@ -490,18 +492,18 @@
     in_my_plane = later & ((dest // CORE) % Z == my_z)
     holder = jnp.max(jnp.where(in_my_plane, dest, 0), axis=1)
     choice = ((holder % CORE) ^ my_core) * X + (my_x - holder // (Z * CORE)) % X
+
+    upper_own, lower_rows = lax.optimization_barrier((gathered(slots, upper), lower_rows))
+    upper_partner = lax.ppermute(upper_own, "grp", mirror)
     lower_send = joined(choice, lower_rows, routed)
     lower = exchanged(lower_send)
-
-    upper_own = gathered(slots, upper)
-    upper_partner = lax.ppermute(upper_own, "grp", mirror)
     lower_own = gathered_lower(slots, jnp.maximum(own_planes, 0), lower)
     lower_partner = lax.ppermute(lower_own, "grp", mirror)
 
     base = plus_own(own_planes, ladder, upper_own, lower_own)
 
     def fast():
-        return minus_mirror(partner_planes, base, upper_partner, lower_partner)
+        return minus_mirror(partner_planes, base, upper_partner, lower_partner, unroll=SIDE)
 
     def slow():
         arrived = exchanged(direct_tiles(direct_blocks, gen_mat, ham_mat))

time: 291 us -> 292 us (level)
  waiting for transfers between devices: 139 us -> 148 us
  starting transfers between devices: 91.2 us -> 82.7 us
    all_to_all x3, waiting for transfers between devices: 14.5 us -> 32.5 us  [exchanged(): lax.all_to_all(value, 'chan', split_axis=0, concat_axis=0, tiled=True)]
    ppermute x14, waiting for transfers between devices: 31.2 us -> 15.5 us  [x_shift(): return lax.ppermute(value, 'chan', pairs)]
    ppermute x1, waiting for transfers between devices: 16.9 us -> 9.11 us  [on_device(): lower_partner = lax.ppermute(lower_own, 'grp', mirror)]
    ppermute x1, waiting for transfers between devices: 0.01 us -> 7.18 us  [on_device(): upper_partner = lax.ppermute(upper_own, 'grp', mirror)]
    ppermute x7, waiting for transfers between devices: 76.6 us -> 83.6 us  [z_shift(): return lax.ppermute(value, 'chan', pairs)]
    ppermute x7, starting transfers between devices: 19.2 us -> 13.1 us  [z_shift(): return lax.ppermute(value, 'chan', pairs)]
  transfers between devices with their start and end apart: 26 -> 26, of which waited for: 9 -> 10; matrix products, arithmetic and copies ran while one was open for 5% -> 5% of each run, Pallas kernels for 4% -> 3%
where the time goes in v3:
time: 292 us; the launch traced here: 291 us
  waiting for transfers between devices  148 us (51%)
  starting transfers between devices  82.7 us (28%)
  Pallas kernels  31.6 us (11%)
  matrix products  12.7 us (4%)
  local copies, waits for them, and re-layouts  7.73 us (3%)
  other arithmetic  7.07 us (2%)
    ppermute x7, waiting for transfers between devices, z_shift(): return lax.ppermute(value, 'chan', pairs)  83.6 us
    ppermute x14, starting transfers between devices, x_shift(): return lax.ppermute(value, 'chan', pairs)  35.6 us
    all_to_all x3, waiting for transfers between devices, exchanged(): lax.all_to_all(value, 'chan', split_axis=0, concat_axis=0, tiled=True)  32.5 us
    all_to_all x3, starting transfers between devices, exchanged(): lax.all_to_all(value, 'chan', split_axis=0, concat_axis=0, tiled=True)  31.3 us
    pallas_call x6, Pallas kernels, kernel_call(): pl.pallas_call(body, out_shape=outs, in_specs=[SMEM] * len(tables) + [HBM...  20.3 us
    ppermute x14, waiting for transfers between devices, x_shift(): return lax.ppermute(value, 'chan', pairs)  15.5 us
    ppermute x7, starting transfers between devices, z_shift(): return lax.ppermute(value, 'chan', pairs)  13.1 us
    pallas_call x2, Pallas kernels, by_bands(): pl.pallas_call(body, grid=(SIDE,), out_shape=kind((side, side), F32), in_...  11.3 us
  transfers between devices with their start and end apart: 26, of which 10 were waited for; matrix products, arithmetic and copies ran while one was open for 5% of the time, Pallas kernels for 3%

profile of v3, /device:TPU:1, one launch (start us, length us, event | category | flops | bytes accessed | tf_op | source)
XLA Modules:
  0.0 291.0 jit_solution(18328259992461425619)
XLA Ops:
  1.6 1.8 dynamic-slice_reduce_fusion.1
  4.1 5.0 %shard_map.66 = (bf16[64,2,128,128]{3,2,1,0:T(8,128)(2,1)}, bf16[2,128,128]{2,1,0:T(8,128)(2,1)S(1)}, bf16[2,128,128]{2,1,0:T(8,128)(2,1)S(1)}, bf16[2,128,128]{...) custom-call(s32[64]{0:T(128)S(1)} %select_reduce_fusion.4.main_table, ...), custom_call_target="tpu_custom_call" | custom-call | tf_op jit(solution)/shard_map/pallas_call | solution.py:60
  9.1 13.3 %all-to-all-start.2 = ((bf16[64,2,128,128]{3,2,1,0:T(8,128)(2,1)}), bf16[64,2,128,128]{3,2,1,0:T(8,128)(2,1)}, u32[]{:S(2)}, u32[]{:S(2)}) async-start(bf16[64,2,128,128]{3,2,1,0:T(8,128)(2,1)} %get-tuple-element.101), calls=%async_computation.2 | async-start | bytes 8388608 | tf_op jit(solution)/shard_map/all_to_all | solution.py:53
  22.5 1.4 collective-permute-start.1
  23.9 2.1 collective-permute-start.2
  26.0 2.4 collective-permute-start.3
  28.4 2.1 collective-permute-start.4
  30.4 2.4 collective-permute-start.5
  34.5 2.3 convert_reduce_fusion
  38.1 1.6 select_reduce_fusion.1
  41.3 73.9 %collective-permute-done.1 = bf16[2,128,128]{2,1,0:T(8,128)(2,1)S(1)} collective-permute-done((bf16[2,128,128]{2,1,0:T(8,128)(2,1)S(1)}, bf16[2,128,128]{2,1,0:T(8,128)(2,1)S(1)}, u32[]{:S(2)}, u32[]{:S(2)}) %collective-permute-start.1) | collective-permute-done | bytes 65568 | tf_op jit(solution)/shard_map/ppermute | solution.py:39
  115.2 2.0 collective-permute-start.6
  117.2 2.4 collective-permute-done.2
  120.3 2.1 collective-permute-done.3
  122.5 5.1 %collective-permute-done.4 = bf16[2,128,128]{2,1,0:T(8,128)(2,1)S(1)} collective-permute-done((bf16[2,128,128]{2,1,0:T(8,128)(2,1)S(1)}, bf16[2,128,128]{2,1,0:T(8,128)(2,1)S(1)}, u32[]{:S(2)}, u32[]{:S(2)}) %collective-permute-start.4) | collective-permute-done | bytes 65568 | tf_op jit(solution)/shard_map/ppermute | solution.py:39
  127.7 1.3 collective-permute-start.8
  129.0 2.6 collective-permute-start.9
  131.6 1.1 collective-permute-start.10
  132.9 4.0 %fusion.1 = f32[896,896]{1,0:T(8,128)S(1)} fusion(bf16[1,1,896,896]{3,2,1,0:T(8,128)(2,1)} %param.8, f32[896]{0:T(1024)S(1)} %reduce.1, bf16[1,1,896,896]{3,2,1,0:T(8,128)(2,1)} %param.9), kind=kOutput, calls=%fused_computation.10 | convolution fusion | flops 1441054720 | bytes 6426112 | tf_op jit(solution)/shard_map/dot_general | solution.py:366
  137.0 3.4 %collective-permute-start.11 = (bf16[8,2,128,128]{3,2,1,0:T(8,128)(2,1)S(1)}, bf16[8,2,128,128]{3,2,1,0:T(8,128)(2,1)S(1)}, u32[]{:S(2)}, u32[]{:S(2)}) collective-permute-start(bf16[8,2,128,128]{3,2,1,0:T(8,128)(2,1)S(1)} %bitcast_dynamic-update-slice_fusion.refs_0_), channel_id=1, source_target_pairs={{0,1},{1,0},{2,3},{3,2},{4,5},{5,4},{6,7},{7,6},{8,9},{9,8},{10,11... | collective-permute-start | bytes 1572872 | tf_op jit(solution)/shard_map/ppermute | solution.py:49
  140.4 4.7 %collective-permute-start.12 = (bf16[8,2,128,128]{3,2,1,0:T(8,128)(2,1)S(1)}, bf16[8,2,128,128]{3,2,1,0:T(8,128)(2,1)S(1)}, u32[]{:S(2)}, u32[]{:S(2)}) collective-permute-start(bf16[8,2,128,128]{3,2,1,0:T(8,128)(2,1)S(1)} %collective-permute-done.8.refs_1_), channel_id=1, source_target_pairs={{0,1},{1,0},{2,3},{3,2},{4,5},{5,4},{6,7},{7,6},{8,9},{9,8},{10,11... | collective-permute-start | bytes 1572872 | tf_op jit(solution)/shard_map/ppermute | solution.py:49
  145.2 7.2 %collective-permute-done.9.refs_2_ = bf16[8,2,128,128]{3,2,1,0:T(8,128)(2,1)S(1)} collective-permute-done((bf16[8,2,128,128]{3,2,1,0:T(8,128)(2,1)S(1)}, bf16[8,2,128,128]{3,2,1,0:T(8,128)(2,1)S(1)}, u32[]{:S(2)}, u32[]{:S(2)}) %collective-permute-start.9) | collective-permute-done | bytes 524320 | tf_op jit(solution)/shard_map/ppermute | solution.py:49
  152.4 3.4 %collective-permute-start.13 = (bf16[8,2,128,128]{3,2,1,0:T(8,128)(2,1)S(1)}, bf16[8,2,128,128]{3,2,1,0:T(8,128)(2,1)}, u32[]{:S(2)}, u32[]{:S(2)}) collective-permute-start(bf16[8,2,128,128]{3,2,1,0:T(8,128)(2,1)S(1)} %collective-permute-done.9.refs_2_), channel_id=1, source_target_pairs={{0,1},{1,0},{2,3},{3,2},{4,5},{5,4},{6,7},{7,6},{8,9},{9,8},{10,11... | collective-permute-start | bytes 1572872 | tf_op jit(solution)/shard_map/ppermute | solution.py:49
  155.8 3.7 %convolution_subtract_fusion.1.ladder_ref = f32[896,896]{1,0:T(8,128)} fusion(f32[896,896]{1,0:T(8,128)S(1)} %fusion.1, bf16[1,1,896,896]{3,2,1,0:T(8,128)(2,1)S(1)} %copy-done.14, f32[896]{0:T(1024)S(1)} %reduce.1, bf16[1,1,896,896]{3,2,1,0:T(8,128)(2,1)S(1)} %copy-done.13), kind=kOutput, calls=%fused_computation.8 | convolution fusion | flops 1441857536 | bytes 9637376 | tf_op jit(solution)/shard_map/dot_general | solution.py:367
  159.5 4.3 %shard_map.67 = (bf16[896,896]{1,0:T(8,128)(2,1)S(1)}, bf16[896,896]{1,0:T(8,128)(2,1)S(1)}) custom-call(s32[64]{0:T(128)S(1)} %get-tuple-element.159.main_table, s32[64]{0:T(128)S(1)} %select_reduce_fusion.2.second_table, bf16[64,2,128,128]{3,2,1,0:T(8,128)(2,1)} %all-to-all-done.2.main_ref, ...), custom_call_target="tpu_custom_call" | custom-call | tf_op jit(solution)/shard_map/pallas_call | solution.py:60
  163.9 2.0 fusion.36
  165.9 2.0 convolution_subtract_fusion.cross_ref
  167.9 5.2 %shard_map.68 = (bf16[64,112,128]{2,1,0:T(8,128)(2,1)}, bf16[64,16,128]{2,1,0:T(8,128)(2,1)S(1)}, bf16[64,16,128]{2,1,0:T(8,128)(2,1)S(1)}, bf16[64,16,128]{2,1,...) custom-call(s32[64]{0:T(128)S(1)} %broadcast_maximum_fusion.3.main_t, ...), custom_call_target="tpu_custom_call" | custom-call | tf_op jit(solution)/shard_map/pallas_call | solution.py:60
  174.5 6.7 %all-to-all-start.3 = ((bf16[64,112,128]{2,1,0:T(8,128)(2,1)}), bf16[64,112,128]{2,1,0:T(8,128)(2,1)S(1)}, u32[]{:S(2)}, u32[]{:S(2)}) async-start(bf16[64,112,128]{2,1,0:T(8,128)(2,1)} %get-tuple-element.121), calls=%async_computation.3 | async-start | bytes 3670016 | tf_op jit(solution)/shard_map/all_to_all | solution.py:53
  181.2 1.4 collective-permute-start.15
  182.7 2.6 collective-permute-start.16
  185.3 1.1 collective-permute-start.17
  186.3 1.2 collective-permute-start.18
  187.8 8.3 %collective-permute-done.15.refs_1_ = bf16[64,16,128]{2,1,0:T(8,128)(2,1)S(1)} collective-permute-done((bf16[64,16,128]{2,1,0:T(8,128)(2,1)S(1)}, bf16[64,16,128]{2,1,0:T(8,128)(2,1)S(1)}, u32[]{:S(2)}, u32[]{:S(2)}) %collective-permute-start.15) | collective-permute-done | bytes 262176 | tf_op jit(solution)/shard_map/ppermute | solution.py:49
  196.8 12.4 %collective-permute-start.20 = (bf16[64,16,128]{2,1,0:T(8,128)(2,1)}, bf16[64,16,128]{2,1,0:T(8,128)(2,1)}, u32[]{:S(2)}, u32[]{:S(2)}) collective-permute-start(bf16[64,16,128]{2,1,0:T(8,128)(2,1)} %get-tuple-element.131), channel_id=1, source_target_pairs={{0,33},{1,32},{2,35},{3,34},{4,37},{5,36},{6,39},{7,38},{8,41},{9,... | collective-permute-start | bytes 786440 | tf_op jit(solution)/shard_map/ppermute | solution.py:49
  210.0 16.6 %all-to-all-done.3.main_ref = bf16[64,112,128]{2,1,0:T(8,128)(2,1)S(1)} async-done(((bf16[64,112,128]{2,1,0:T(8,128)(2,1)}), bf16[64,112,128]{2,1,0:T(8,128)(2,1)S(1)}, u32[]{:S(2)}, u32[]{:S(2)}) %all-to-all-start.3) | async-done | bytes 1835040 | tf_op jit(solution)/shard_map/all_to_all | solution.py:53
  226.6 1.2 shard_map.69.upper_ref
  227.9 3.0 %shard_map.70 = bf16[64,32,128]{2,1,0:T(8,128)(2,1)} custom-call(s32[64]{0:T(128)S(1)} %fusion.25.table, bf16[64,16,128]{2,1,0:T(8,128)(2,1)S(1)} %copy-done.5, bf16[64,16,128]{2,1,0:T(8,128)(2,1)S(1)} %copy-done.7, bf16[64,16,128]{2,1,0:T(8,128)(2,1)S(1)} %copy-done.9, bf16[64,16,128]{2,1,0:T(8,128)(2,1)S(1)} %copy-done.11, ...), custom_call_target="tpu_custom_call" | custom-call | tf_op jit(solution)/shard_map/pallas_call | solution.py:60
  231.0 11.3 %all-to-all-start.4 = ((bf16[64,32,128]{2,1,0:T(8,128)(2,1)}), bf16[64,32,128]{2,1,0:T(8,128)(2,1)S(1)}, u32[]{:S(2)}, u32[]{:S(2)}) async-start(bf16[64,32,128]{2,1,0:T(8,128)(2,1)} %shard_map.70), calls=%async_computation.4 | async-start | bytes 1048576 | tf_op jit(solution)/shard_map/all_to_all | solution.py:53
  242.2 1.4 collective-permute-start.22
  243.6 15.9 %all-to-all-done.4.main_ref = bf16[64,32,128]{2,1,0:T(8,128)(2,1)S(1)} async-done(((bf16[64,32,128]{2,1,0:T(8,128)(2,1)}), bf16[64,32,128]{2,1,0:T(8,128)(2,1)S(1)}, u32[]{:S(2)}, u32[]{:S(2)}) %all-to-all-start.4) | async-done | bytes 524320 | tf_op jit(solution)/shard_map/all_to_all | solution.py:53
  259.5 1.5 shard_map.71.lower_ref
  261.0 1.4 collective-permute-start.23
  262.5 4.7 %shard_map.72 = f32[896,896]{1,0:T(8,128)S(1)} custom-call(s32[49]{0:T(128)S(1)} %get-tuple-element.106.table, f32[896,896]{1,0:T(8,128)} %convolution_subtract_fusion.1.ladder_ref, bf16[49,112,128]{2,1,0:T(8,128)(2,1)S(1)} %shard_map.69.upper_ref, bf16[105,16,128]{2,1,0:T(8,128)(2,1)S(1)} %shard_map.71.lower_ref), custom_call_target="tpu_custom_call" | custom-call | tf_op jit(solution)/shard_map/pallas_call | solution.py:325
  267.2 7.2 %collective-permute-done.22 = bf16[49,112,128]{2,1,0:T(8,128)(2,1)} collective-permute-done((bf16[49,112,128]{2,1,0:T(8,128)(2,1)S(1)}, bf16[49,112,128]{2,1,0:T(8,128)(2,1)}, u32[]{:S(2)}, u32[]{:S(2)}) %collective-permute-start.22) | collective-permute-done | bytes 1404960 | tf_op jit(solution)/shard_map/ppermute | solution.py:497
  274.3 9.1 %collective-permute-done.23 = bf16[105,16,128]{2,1,0:T(8,128)(2,1)S(1)} collective-permute-done((bf16[105,16,128]{2,1,0:T(8,128)(2,1)S(1)}, bf16[105,16,128]{2,1,0:T(8,128)(2,1)S(1)}, u32[]{:S(2)}, u32[]{:S(2)}) %collective-permute-start.23) | collective-permute-done | bytes 430112 | tf_op jit(solution)/shard_map/ppermute | solution.py:501
  283.4 6.6 %conditional.1 = (f32[1,1,896,896]{3,2,1,0:T(8,128)}) conditional(s32[]{:T(128)} %convert_element_type.63, (s32[49]{0:T(128)S(1)}, f32[896,896]{1,0:T(8,128)S(1)}, bf16[49,112,128]{2,1,0:T(8,128)(2,1)}, bf16[105,16,128]{2,1,0:T(8,128)(2,1)S(1)}) %tuple.19, (s32[49]{0:T(128)S(1)}, pred[49]{0:T(512)(128)(4,1)S(1)}, s32[64]{0:T(128)S(1)}, ...), branch_computations={%region_19.20_spmd, %region_20.22_spmd} | conditional | flops 9555 | bytes 78049072 | solution.py:519
  283.4 6.6 %branch_0_fun.1 = f32[896,896]{1,0:T(8,128)} custom-call(s32[49]{0:T(128)S(1)} %get-tuple-element.47.table, f32[896,896]{1,0:T(8,128)S(1)} %get-tuple-element.48.base_ref, bf16[49,112,128]{2,1,0:T(8,128)(2,1)} %get-tuple-element.49.upper_ref, bf16[105,16,128]{2,1,0:T(8,128)(2,1)S(1)} %get-tuple-element.50.lower_ref), custom_call_target="tpu_custom_call" | custom-call | tf_op jit(solution)/shard_map/cond/branch_0_fun/pallas_call | solution.py:325
  (105 shorter events, 11.2 us)
Async XLA Ops:
  0.0 34.4 %copy-start = (s32[4,64,49]{1,0,2:T(4,128)S(1)}, s32[4,64,49]{1,0,2:T(4,128)}, u32[]{:S(2)}) copy-start(s32[4,64,49]{1,0,2:T(4,128)} %param.12) | copy-start | bytes 150532
  9.1 23.7 %copy-start.15 = (s32[4,64,49,1]{1,3,2,0:T(1,128)S(1)}, s32[4,64,49,1]{1,3,2,0:T(1,128)}, u32[]{:S(2)}) copy-start(s32[4,64,49,1]{1,3,2,0:T(1,128)} %param.11) | copy-start | bytes 150532
  9.1 32.1 %copy-start.16 = (f32[1,1,896]{2,1,0:T(1,128)S(1)}, f32[1,1,896]{2,1,0:T(1,128)}, u32[]{:S(2)}) copy-start(f32[1,1,896]{2,1,0:T(1,128)} %param.10) | copy-start | bytes 10756
  9.1 150.3 %all-to-all-start.2 = ((bf16[64,2,128,128]{3,2,1,0:T(8,128)(2,1)}), bf16[64,2,128,128]{3,2,1,0:T(8,128)(2,1)}, u32[]{:S(2)}, u32[]{:S(2)}) async-start(bf16[64,2,128,128]{3,2,1,0:T(8,128)(2,1)} %get-tuple-element.101), calls=%async_computation.2 | async-start | bytes 8388608 | tf_op jit(solution)/shard_map/all_to_all | solution.py:53
  22.5 92.7 %collective-permute-start.1 = (bf16[2,128,128]{2,1,0:T(8,128)(2,1)S(1)}, bf16[2,128,128]{2,1,0:T(8,128)(2,1)S(1)}, u32[]{:S(2)}, u32[]{:S(2)}) collective-permute-start(bf16[2,128,128]{2,1,0:T(8,128)(2,1)S(1)} %get-tuple-element.112), channel_id=1, source_target_pairs={{0,2},{1,3},{2,4},{3,5},{4,6},{5,7},{6,8},{7,9},{8,10},{9,11},{10,... | collective-permute-start | bytes 196616 | tf_op jit(solution)/shard_map/ppermute | solution.py:39
  23.9 95.7 %collective-permute-start.2 = (bf16[2,128,128]{2,1,0:T(8,128)(2,1)S(1)}, bf16[2,128,128]{2,1,0:T(8,128)(2,1)S(1)}, u32[]{:S(2)}, u32[]{:S(2)}) collective-permute-start(bf16[2,128,128]{2,1,0:T(8,128)(2,1)S(1)} %get-tuple-element.113), channel_id=1, source_target_pairs={{0,4},{1,5},{2,6},{3,7},{4,8},{5,9},{6,10},{7,11},{8,12},{9,13},{1... | collective-permute-start | bytes 196616 | tf_op jit(solution)/shard_map/ppermute | solution.py:39
  26.0 96.5 %collective-permute-start.3 = (bf16[2,128,128]{2,1,0:T(8,128)(2,1)S(1)}, bf16[2,128,128]{2,1,0:T(8,128)(2,1)S(1)}, u32[]{:S(2)}, u32[]{:S(2)}) collective-permute-start(bf16[2,128,128]{2,1,0:T(8,128)(2,1)S(1)} %get-tuple-element.114), channel_id=1, source_target_pairs={{0,6},{1,7},{2,8},{3,9},{4,10},{5,11},{6,12},{7,13},{8,14},{9,15},... | collective-permute-start | bytes 196616 | tf_op jit(solution)/shard_map/ppermute | solution.py:39
  28.4 99.2 %collective-permute-start.4 = (bf16[2,128,128]{2,1,0:T(8,128)(2,1)S(1)}, bf16[2,128,128]{2,1,0:T(8,128)(2,1)S(1)}, u32[]{:S(2)}, u32[]{:S(2)}) collective-permute-start(bf16[2,128,128]{2,1,0:T(8,128)(2,1)S(1)} %get-tuple-element.115), channel_id=1, source_target_pairs={{0,8},{1,9},{2,10},{3,11},{4,12},{5,13},{6,14},{7,15},{8,0},{9,1},... | collective-permute-start | bytes 196616 | tf_op jit(solution)/shard_map/ppermute | solution.py:39
  30.4 97.2 %collective-permute-start.5 = (bf16[2,128,128]{2,1,0:T(8,128)(2,1)S(1)}, bf16[2,128,128]{2,1,0:T(8,128)(2,1)S(1)}, u32[]{:S(2)}, u32[]{:S(2)}) collective-permute-start(bf16[2,128,128]{2,1,0:T(8,128)(2,1)S(1)} %get-tuple-element.116), channel_id=1, source_target_pairs={{0,10},{1,11},{2,12},{3,13},{4,14},{5,15},{6,0},{7,1},{8,2},{9,3},... | collective-permute-start | bytes 196616 | tf_op jit(solution)/shard_map/ppermute | solution.py:39
  115.2 12.5 %collective-permute-start.6 = (bf16[2,128,128]{2,1,0:T(8,128)(2,1)S(1)}, bf16[2,128,128]{2,1,0:T(8,128)(2,1)S(1)}, u32[]{:S(2)}, u32[]{:S(2)}) collective-permute-start(bf16[2,128,128]{2,1,0:T(8,128)(2,1)S(1)} %get-tuple-element.117), channel_id=1, source_target_pairs={{0,12},{1,13},{2,14},{3,15},{4,0},{5,1},{6,2},{7,3},{8,4},{9,5},{1... | collective-permute-start | bytes 196616 | tf_op jit(solution)/shard_map/ppermute | solution.py:39
  119.6 8.1 %collective-permute-start.7 = (bf16[2,128,128]{2,1,0:T(8,128)(2,1)S(1)}, bf16[2,128,128]{2,1,0:T(8,128)(2,1)S(1)}, u32[]{:S(2)}, u32[]{:S(2)}) collective-permute-start(bf16[2,128,128]{2,1,0:T(8,128)(2,1)S(1)} %get-tuple-element.118), channel_id=1, source_target_pairs={{0,14},{1,15},{2,0},{3,1},{4,2},{5,3},{6,4},{7,5},{8,6},{9,7},{10,... | collective-permute-start | bytes 196616 | tf_op jit(solution)/shard_map/ppermute | solution.py:39
  127.7 12.7 %collective-permute-start.8 = (bf16[8,2,128,128]{3,2,1,0:T(8,128)(2,1)S(1)}, bf16[8,2,128,128]{3,2,1,0:T(8,128)(2,1)S(1)}, u32[]{:S(2)}, u32[]{:S(2)}) collective-permute-start(bf16[8,2,128,128]{3,2,1,0:T(8,128)(2,1)S(1)} %bitcast_dynamic-update-slice_fusion.refs_0_), channel_id=1, source_target_pairs={{0,16},{1,17},{2,18},{3,19},{4,20},{5,21},{6,22},{7,23},{8,24},{9,... | collective-permute-start | bytes 1572872 | tf_op jit(solution)/shard_map/ppermute | solution.py:49
  129.0 23.3 %collective-permute-start.9 = (bf16[8,2,128,128]{3,2,1,0:T(8,128)(2,1)S(1)}, bf16[8,2,128,128]{3,2,1,0:T(8,128)(2,1)S(1)}, u32[]{:S(2)}, u32[]{:S(2)}) collective-permute-start(bf16[8,2,128,128]{3,2,1,0:T(8,128)(2,1)S(1)} %bitcast_dynamic-update-slice_fusion.refs_0_), channel_id=1, source_target_pairs={{0,32},{1,33},{2,34},{3,35},{4,36},{5,37},{6,38},{7,39},{8,40},{9,... | collective-permute-start | bytes 1572872 | tf_op jit(solution)/shard_map/ppermute | solution.py:49
  131.6 24.1 %collective-permute-start.10 = (bf16[8,2,128,128]{3,2,1,0:T(8,128)(2,1)S(1)}, bf16[8,2,128,128]{3,2,1,0:T(8,128)(2,1)S(1)}, u32[]{:S(2)}, u32[]{:S(2)}) collective-permute-start(bf16[8,2,128,128]{3,2,1,0:T(8,128)(2,1)S(1)} %bitcast_dynamic-update-slice_fusion.refs_0_), channel_id=1, source_target_pairs={{0,48},{1,49},{2,50},{3,51},{4,52},{5,53},{6,54},{7,55},{8,56},{9,... | collective-permute-start | bytes 1572872 | tf_op jit(solution)/shard_map/ppermute | solution.py:49
  132.9 22.9 %copy-start.13 = (bf16[1,1,896,896]{3,2,1,0:T(8,128)(2,1)S(1)}, bf16[1,1,896,896]{3,2,1,0:T(8,128)(2,1)}, u32[]{:S(2)}) copy-start(bf16[1,1,896,896]{3,2,1,0:T(8,128)(2,1)} %param.8) | copy-start | bytes 4816900
  132.9 22.9 %copy-start.14 = (bf16[1,1,896,896]{3,2,1,0:T(8,128)(2,1)S(1)}, bf16[1,1,896,896]{3,2,1,0:T(8,128)(2,1)}, u32[]{:S(2)}) copy-start(bf16[1,1,896,896]{3,2,1,0:T(8,128)(2,1)} %param.9) | copy-start | bytes 4816900
  137.0 22.5 %collective-permute-start.11 = (bf16[8,2,128,128]{3,2,1,0:T(8,128)(2,1)S(1)}, bf16[8,2,128,128]{3,2,1,0:T(8,128)(2,1)S(1)}, u32[]{:S(2)}, u32[]{:S(2)}) collective-permute-start(bf16[8,2,128,128]{3,2,1,0:T(8,128)(2,1)S(1)} %bitcast_dynamic-update-slice_fusion.refs_0_), channel_id=1, source_target_pairs={{0,1},{1,0},{2,3},{3,2},{4,5},{5,4},{6,7},{7,6},{8,9},{9,8},{10,11... | collective-permute-start | bytes 1572872 | tf_op jit(solution)/shard_map/ppermute | solution.py:49
  140.4 19.1 %collective-permute-start.12 = (bf16[8,2,128,128]{3,2,1,0:T(8,128)(2,1)S(1)}, bf16[8,2,128,128]{3,2,1,0:T(8,128)(2,1)S(1)}, u32[]{:S(2)}, u32[]{:S(2)}) collective-permute-start(bf16[8,2,128,128]{3,2,1,0:T(8,128)(2,1)S(1)} %collective-permute-done.8.refs_1_), channel_id=1, source_target_pairs={{0,1},{1,0},{2,3},{3,2},{4,5},{5,4},{6,7},{7,6},{8,9},{9,8},{10,11... | collective-permute-start | bytes 1572872 | tf_op jit(solution)/shard_map/ppermute | solution.py:49
  152.4 7.1 %collective-permute-start.13 = (bf16[8,2,128,128]{3,2,1,0:T(8,128)(2,1)S(1)}, bf16[8,2,128,128]{3,2,1,0:T(8,128)(2,1)}, u32[]{:S(2)}, u32[]{:S(2)}) collective-permute-start(bf16[8,2,128,128]{3,2,1,0:T(8,128)(2,1)S(1)} %collective-permute-done.9.refs_2_), channel_id=1, source_target_pairs={{0,1},{1,0},{2,3},{3,2},{4,5},{5,4},{6,7},{7,6},{8,9},{9,8},{10,11... | collective-permute-start | bytes 1572872 | tf_op jit(solution)/shard_map/ppermute | solution.py:49
  155.8 3.8 %collective-permute-start.14 = (bf16[8,2,128,128]{3,2,1,0:T(8,128)(2,1)S(1)}, bf16[8,2,128,128]{3,2,1,0:T(8,128)(2,1)}, u32[]{:S(2)}, u32[]{:S(2)}) collective-permute-start(bf16[8,2,128,128]{3,2,1,0:T(8,128)(2,1)S(1)} %collective-permute-done.10.refs_3_), channel_id=1, source_target_pairs={{0,1},{1,0},{2,3},{3,2},{4,5},{5,4},{6,7},{7,6},{8,9},{9,8},{10,11... | collective-permute-start | bytes 1572872 | tf_op jit(solution)/shard_map/ppermute | solution.py:49
  173.1 0.7 copy-start.4
  173.8 0.7 copy-start.6
  174.5 6.7 %copy-start.18 = (bf16[64,16,128]{2,1,0:T(8,128)(2,1)S(1)}, bf16[64,16,128]{2,1,0:T(8,128)(2,1)}, u32[]{:S(2)}) copy-start(bf16[64,16,128]{2,1,0:T(8,128)(2,1)} %get-tuple-element.126) | copy-start | bytes 786436
  174.5 8.2 %copy-start.17 = (bf16[64,16,128]{2,1,0:T(8,128)(2,1)S(1)}, bf16[64,16,128]{2,1,0:T(8,128)(2,1)}, u32[]{:S(2)}) copy-start(bf16[64,16,128]{2,1,0:T(8,128)(2,1)} %get-tuple-element.127) | copy-start | bytes 786436
  174.5 52.1 %all-to-all-start.3 = ((bf16[64,112,128]{2,1,0:T(8,128)(2,1)}), bf16[64,112,128]{2,1,0:T(8,128)(2,1)S(1)}, u32[]{:S(2)}, u32[]{:S(2)}) async-start(bf16[64,112,128]{2,1,0:T(8,128)(2,1)} %get-tuple-element.121), calls=%async_computation.3 | async-start | bytes 3670016 | tf_op jit(solution)/shard_map/all_to_all | solution.py:53
  181.2 14.9 %collective-permute-start.15 = (bf16[64,16,128]{2,1,0:T(8,128)(2,1)S(1)}, bf16[64,16,128]{2,1,0:T(8,128)(2,1)S(1)}, u32[]{:S(2)}, u32[]{:S(2)}) collective-permute-start(bf16[64,16,128]{2,1,0:T(8,128)(2,1)S(1)} %copy-done.18), channel_id=1, source_target_pairs={{0,16},{1,17},{2,18},{3,19},{4,20},{5,21},{6,22},{7,23},{8,24},{9,... | collective-permute-start | bytes 786440 | tf_op jit(solution)/shard_map/ppermute | solution.py:49
  182.7 26.6 %collective-permute-start.16 = (bf16[64,16,128]{2,1,0:T(8,128)(2,1)S(1)}, bf16[64,16,128]{2,1,0:T(8,128)(2,1)S(1)}, u32[]{:S(2)}, u32[]{:S(2)}) collective-permute-start(bf16[64,16,128]{2,1,0:T(8,128)(2,1)S(1)} %copy-done.17), channel_id=1, source_target_pairs={{0,32},{1,33},{2,34},{3,35},{4,36},{5,37},{6,38},{7,39},{8,40},{9,... | collective-permute-start | bytes 786440 | tf_op jit(solution)/shard_map/ppermute | solution.py:49
  185.3 42.6 %collective-permute-start.17 = (bf16[64,16,128]{2,1,0:T(8,128)(2,1)}, bf16[64,16,128]{2,1,0:T(8,128)(2,1)}, u32[]{:S(2)}, u32[]{:S(2)}) collective-permute-start(bf16[64,16,128]{2,1,0:T(8,128)(2,1)} %get-tuple-element.128), channel_id=1, source_target_pairs={{0,48},{1,49},{2,50},{3,51},{4,52},{5,53},{6,54},{7,55},{8,56},{9,... | collective-permute-start | bytes 786440 | tf_op jit(solution)/shard_map/ppermute | solution.py:49
  186.3 41.5 %collective-permute-start.18 = (bf16[64,16,128]{2,1,0:T(8,128)(2,1)}, bf16[64,16,128]{2,1,0:T(8,128)(2,1)}, u32[]{:S(2)}, u32[]{:S(2)}) collective-permute-start(bf16[64,16,128]{2,1,0:T(8,128)(2,1)} %get-tuple-element.129), channel_id=1, source_target_pairs={{0,1},{1,0},{2,3},{3,2},{4,5},{5,4},{6,7},{7,6},{8,9},{9,8},{10,11... | collective-permute-start | bytes 786440 | tf_op jit(solution)/shard_map/ppermute | solution.py:49
  187.6 40.3 %collective-permute-start.19 = (bf16[64,16,128]{2,1,0:T(8,128)(2,1)}, bf16[64,16,128]{2,1,0:T(8,128)(2,1)}, u32[]{:S(2)}, u32[]{:S(2)}) collective-permute-start(bf16[64,16,128]{2,1,0:T(8,128)(2,1)} %get-tuple-element.130), channel_id=1, source_target_pairs={{0,17},{1,16},{2,19},{3,18},{4,21},{5,20},{6,23},{7,22},{8,25},{9,... | collective-permute-start | bytes 786440 | tf_op jit(solution)/shard_map/ppermute | solution.py:49
  196.1 0.7 copy-start.8
  196.8 31.1 %collective-permute-start.20 = (bf16[64,16,128]{2,1,0:T(8,128)(2,1)}, bf16[64,16,128]{2,1,0:T(8,128)(2,1)}, u32[]{:S(2)}, u32[]{:S(2)}) collective-permute-start(bf16[64,16,128]{2,1,0:T(8,128)(2,1)} %get-tuple-element.131), channel_id=1, source_target_pairs={{0,33},{1,32},{2,35},{3,34},{4,37},{5,36},{6,39},{7,38},{8,41},{9,... | collective-permute-start | bytes 786440 | tf_op jit(solution)/shard_map/ppermute | solution.py:49
  209.3 0.7 copy-start.10
  210.0 17.9 %collective-permute-start.21 = (bf16[64,16,128]{2,1,0:T(8,128)(2,1)}, bf16[64,16,128]{2,1,0:T(8,128)(2,1)}, u32[]{:S(2)}, u32[]{:S(2)}) collective-permute-start(bf16[64,16,128]{2,1,0:T(8,128)(2,1)} %get-tuple-element.132), channel_id=1, source_target_pairs={{0,49},{1,48},{2,51},{3,50},{4,53},{5,52},{6,55},{7,54},{8,57},{9,... | collective-permute-start | bytes 786440 | tf_op jit(solution)/shard_map/ppermute | solution.py:49
  226.6 1.3 copy-start.5
  226.6 1.3 copy-start.7
  226.6 1.3 copy-start.9
  226.6 1.3 copy-start.11
  231.0 28.6 %all-to-all-start.4 = ((bf16[64,32,128]{2,1,0:T(8,128)(2,1)}), bf16[64,32,128]{2,1,0:T(8,128)(2,1)S(1)}, u32[]{:S(2)}, u32[]{:S(2)}) async-start(bf16[64,32,128]{2,1,0:T(8,128)(2,1)} %shard_map.70), calls=%async_computation.4 | async-start | bytes 1048576 | tf_op jit(solution)/shard_map/all_to_all | solution.py:53
  242.2 32.1 %collective-permute-start.22 = (bf16[49,112,128]{2,1,0:T(8,128)(2,1)S(1)}, bf16[49,112,128]{2,1,0:T(8,128)(2,1)}, u32[]{:S(2)}, u32[]{:S(2)}) collective-permute-start(bf16[49,112,128]{2,1,0:T(8,128)(2,1)S(1)} %shard_map.69.upper_ref), channel_id=1, source_target_pairs={{0,64},{64,0},{128,192},{192,128},{1,65},{65,1},{129,193},{193,129... | collective-permute-start | bytes 4214792 | tf_op jit(solution)/shard_map/ppermute | solution.py:497
  261.0 22.4 %collective-permute-start.23 = (bf16[105,16,128]{2,1,0:T(8,128)(2,1)S(1)}, bf16[105,16,128]{2,1,0:T(8,128)(2,1)S(1)}, u32[]{:S(2)}, u32[]{:S(2)}) collective-permute-start(bf16[105,16,128]{2,1,0:T(8,128)(2,1)S(1)} %shard_map.71.lower_ref), channel_id=1, source_target_pairs={{0,64},{64,0},{128,192},{192,128},{1,65},{65,1},{129,193},{193,129... | collective-permute-start | bytes 1290248 | tf_op jit(solution)/shard_map/ppermute | solution.py:501
  290.1 0.9 copy-start.1
